TPU v7x, 256 devices: a whole 4x4x8 slice. The times are simulated.
256 devices in a mesh: rows: 128 (over z, x, y), cols: 2 (over core).
Axes of the slice: x: 4, y: 4, z: 8, core: 2. Of those that a mesh axis runs over, the one named last changes fastest.
Arguments:
- friction: float32 [4096, 8192], P('rows', 'cols'), may hold values from 0.00015625 to 0.015625
- sources: int32 [4096, 8192], P('rows', 'cols'), may hold values from 0 to 1, as said below
Outputs:
- cost: float32 [4096, 8192], P('rows', 'cols')
- overview_one: float32 [2048, 4096], P('rows', 'cols')
- overview_two: float32 [1024, 2048], P('rows', 'cols')
- change: float32 [1], replicated
Inputs may be any that keep to these rules, and one draw needn't show every extreme that they name: `sources`: at least one cell of the raster is a source.
All inputs are finite; a program needn't handle non-finite values.
Results may differ from a plain program's by a relative error of at most 0.00002.
Values sent between devices are 32-bit elements; how exact they have to be, the bound alone decides.
A program may use at most 128 MiB of HBM per device.

v0:
```python
import functools

import jax
import jax.numpy as jnp
from jax import lax
from jax.experimental import pallas as pl
from jax.experimental.pallas import tpu as pltpu
from jax.sharding import PartitionSpec as P

HUGE = 1e30
MESH = pl.DeviceIdType.MESH
ROWS = 32
CHUNKS = 32
LANES = 128
PLANE = 16


def kernel(
    nz, np_, f_hbm, s_hbm, cost_hbm, one_hbm, two_hbm, change_ref,
    fn, sn, h_ref, x_ref, d_ref, u_ref, ht, xt, vf, vb, on, pool, o1, o2,
    s1a, r1a, s2a, r2a, s1b, r1b, s2b, r2b, s3, r3, pre, enter, xs, xr,
    in_sem, out_sem, send1, recv1, send2, recv2, send3, recv3, sendx, recvx,
):
    width = CHUNKS // np_
    row = lax.axis_index("rows")
    core = lax.axis_index("cols")
    z, p = row // np_, row % np_
    tile = (4, 8, LANES)
    part = (width, LANES)

    in_f = pltpu.make_async_copy(f_hbm, fn, in_sem.at[0])
    in_s = pltpu.make_async_copy(s_hbm, sn, in_sem.at[1])
    in_f.start()
    in_s.start()

    def in_plane(k):
        return (z * np_ + (p + k) % np_, core)

    def in_z(k):
        return (((z + k) % nz) * np_ + p, core)

    barrier = pltpu.get_barrier_semaphore()
    for k in range(1, np_):
        pl.semaphore_signal(barrier, inc=1, device_id=in_plane(k), device_id_type=MESH)
    for k in range(1, nz):
        pl.semaphore_signal(barrier, inc=1, device_id=in_z(k), device_id_type=MESH)
    pl.semaphore_signal(barrier, inc=1, device_id=(row, 1 - core), device_id_type=MESH)

    huge = jnp.full(tile, HUGE, jnp.float32)
    zero = jnp.zeros(tile, jnp.float32)

    in_f.wait()
    in_s.wait()

    def spread(b, _):
        for s in range(8):
            for g in range(4):
                lines = pl.ds((b * 32 + g * 8) * 8 + s, 8, stride=8)
                h_ref[b * 8 + s, g] = 0.5 * fn[lines, :]
                x_ref[b * 8 + s, g] = jnp.where(sn[lines, :] == 1, 0.0, HUGE)
        return 0

    lax.fori_loop(0, ROWS // 8, spread, 0)

    def first_local(b, carry):
        down, up, hd, hu, total = carry
        for s in range(8):
            i = b * 8 + s
            h = h_ref[i]
            down = jnp.minimum(x_ref[i], down + (hd + h))
            total = total + h
            hd = h
            h = h_ref[ROWS - 1 - i]
            up = jnp.minimum(x_ref[ROWS - 1 - i], up + (hu + h))
            hu = h
        return (down, up, hd, hu, total)

    def second_local(b, carry):
        down, up, hd, hu, far_d, far_u, most = carry
        for s in range(8):
            i = b * 8 + s
            h, x = h_ref[i], x_ref[i]
            down = jnp.minimum(x, down + (hd + h))
            far_d = jnp.maximum(x, far_d - (hd + h))
            most = jnp.maximum(most, x - down)
            hd = h
            h, x = h_ref[ROWS - 1 - i], x_ref[ROWS - 1 - i]
            up = jnp.minimum(x, up + (hu + h))
            far_u = jnp.maximum(x, far_u - (hu + h))
            most = jnp.maximum(most, x - up)
            hu = h
        return (down, up, hd, hu, far_d, far_u, most)

    def put(to, item, value):
        for q in range(np_):
            line = q * width
            to[q, item] = value[line // 8, line % 8 : line % 8 + width, :]

    def exchange(to, got, peer, count, mine, sends, recvs):
        copies = []
        for k in range(1, count):
            target = (mine + k) % count
            copy = pltpu.make_async_remote_copy(
                src_ref=to.at[target],
                dst_ref=got.at[mine],
                send_sem=sends.at[k],
                recv_sem=recvs.at[k],
                device_id=peer(k),
                device_id_type=MESH,
            )
            copy.start()
            copies.append(copy)
        return copies

    def finish(copies):
        for copy in copies:
            copy.wait()

    my_z = jnp.full(part, z, jnp.int32)

    def pick(k, new, old):
        return jnp.where(my_z == k, new, old)

    def vertical(step):
        s1, r1, s2, r2 = ((s1a, r1a, s2a, r2a), (s1b, r1b, s2b, r2b))[step]
        if step == 0:
            down, up, hd, hu, total = lax.fori_loop(
                0, ROWS // 8, first_local, (huge, huge, zero, zero, zero)
            )
            values = (up + hu, down + hd, 2.0 * total)
        else:
            down, up, hd, hu, far_d, far_u, most = lax.fori_loop(
                0, ROWS // 8, second_local, (huge, huge, zero, zero, -huge, -huge, zero)
            )
            values = (up + hu, down + hd, far_u - hu, far_d - hd, most)
        items = len(values)
        for item, value in enumerate(values):
            put(s1, item, value)
        if step == 0:
            pl.semaphore_wait(barrier, np_ + nz - 1)
        copies = exchange(s1, r1, in_plane, np_, p, send1.at[step], recv1.at[step])
        for item in range(items):
            r1[p, item] = s1[p, item]
        finish(copies)

        near = jnp.full(part, HUGE, jnp.float32)
        none = jnp.zeros(part, jnp.float32)
        b, a, s_down, s_up, far_d, far_u, most = near, near, none, none, -near, -near, none
        for q in range(np_):
            r_a, r_b = r1[q, 0], r1[q, 1]
            if step == 0:
                s = r1[q, 2]
                pre[q, 2] = s_down
                s_down = s_down + s
            else:
                s = r1a[q, 2]
                most = jnp.maximum(most, jnp.maximum(far_d - r_a, r1[q, 2] - b))
                most = jnp.maximum(most, r1[q, 4])
                far_d = jnp.maximum(r1[q, 3], far_d - s)
            pre[q, 0] = b
            b = jnp.minimum(r_b, b + s)
        for q in range(np_ - 1, -1, -1):
            s = r1a[q, 2]
            if step == 0:
                pre[q, 3] = s_up
                s_up = s_up + s
            else:
                far_u = jnp.maximum(r1[q, 2], far_u - s)
            pre[q, 1] = a
            a = jnp.minimum(r1[q, 0], a + s)
        values = (a, b, s_down) if step == 0 else (a, b, far_u, far_d, most)
        for k in range(nz):
            for item, value in enumerate(values):
                s2[k, item] = value
        copies = exchange(s2, r2, in_z, nz, z, send2.at[step], recv2.at[step])
        for item in range(items):
            r2[z, item] = values[item]
        finish(copies)

        b, a, far_d, most = near, near, -near, none
        in_d, in_u = near, near
        for k in range(nz):
            in_d = pick(k, b, in_d)
            s = r2a[k, 2]
            if step == 1:
                most = jnp.maximum(most, jnp.maximum(far_d - r2[k, 0], r2[k, 2] - b))
                most = jnp.maximum(most, r2[k, 4])
                far_d = jnp.maximum(r2[k, 3], far_d - s)
            b = jnp.minimum(r2[k, 1], b + s)
        for k in range(nz - 1, -1, -1):
            in_u = pick(k, a, in_u)
            a = jnp.minimum(r2[k, 0], a + r2a[k, 2])
        to, got = s3.at[step], r3.at[step]
        for q in range(np_):
            to[q, 0] = jnp.minimum(pre[q, 0], in_d + pre[q, 2])
            to[q, 1] = jnp.minimum(pre[q, 1], in_u + pre[q, 3])
            to[q, 2] = most
        copies = exchange(to, got, in_plane, np_, p, send3.at[step], recv3.at[step])
        for item in range(3):
            got[p, item] = to[p, item]
        finish(copies)
        most = got[0, 2]
        for q in range(np_):
            line = q * width
            for item in range(2):
                enter[item, line // 8, line % 8 : line % 8 + width, :] = got[q, item]
            most = jnp.maximum(most, got[q, 2])

        def final(b, carry):
            down, up, hd, hu = carry
            for s in range(8):
                i = b * 8 + s
                h = h_ref[i]
                down = jnp.minimum(x_ref[i], down + (hd + h))
                d_ref[i] = down
                hd = h
                h = h_ref[ROWS - 1 - i]
                up = jnp.minimum(x_ref[ROWS - 1 - i], up + (hu + h))
                u_ref[ROWS - 1 - i] = up
                hu = h
            return (down, up, hd, hu)

        lax.fori_loop(0, ROWS // 8, final, (enter[0], enter[1], zero, zero))
        return most

    lane = lax.broadcasted_iota(jnp.int32, (8, LANES), 1)
    sub = lax.broadcasted_iota(jnp.int32, (8, LANES), 0)
    inner, outer = lane % 8, sub % 4
    huge2 = jnp.full((8, LANES), HUGE, jnp.float32)
    zero2 = jnp.zeros((8, LANES), jnp.float32)

    def block(load, j):
        return load(pl.ds((j // 4) * 16, 16), j % 4).reshape(LANES, LANES)

    def scan_all(c, s, axis, size, place, forward):
        step = 1 if forward else -1
        extent = c.shape[axis]
        at = place if forward else size - 1 - place
        run, length = huge2, zero2
        for k in range(size - 1, 0, -1):
            ck = pltpu.roll(c, (step * k) % extent, axis)
            sk = pltpu.roll(s, (step * k) % extent, axis)
            here = at >= k
            run = jnp.where(here, jnp.minimum(ck, run + sk), run)
            length = jnp.where(here, length + sk, length)
        before, passed = run, length
        run, length = jnp.minimum(c, run + s), length + s
        for k in range(1, size):
            ck = pltpu.roll(c, (-step * k) % extent, axis)
            sk = pltpu.roll(s, (-step * k) % extent, axis)
            here = at + k < size
            run = jnp.where(here, jnp.minimum(ck, run + sk), run)
            length = jnp.where(here, length + sk, length)
        return before, passed, run, length

    def horizontal(step, most):
        for j in range(8):
            rows = pl.ds(j, LANES, stride=8)
            xt[rows, :] = block(lambda r, g: jnp.minimum(d_ref[r, g], u_ref[r, g]), j).T
            if step == 0:
                ht[rows, :] = block(lambda r, g: h_ref[r, g], j).T

        def at(i):
            return pl.ds(pl.multiple_of(i * 8, 8), 8)

        def local(b, carry):
            right, left, hr, hl, total = carry
            for s in range(8):
                i = b * 8 + s
                h = ht[at(i), :]
                right = jnp.minimum(xt[at(i), :], right + (hr + h))
                total = total + h
                hr = h
                h = ht[at(LANES - 1 - i), :]
                left = jnp.minimum(xt[at(LANES - 1 - i), :], left + (hl + h))
                hl = h
            return (right, left, hr, hl, total)

        right, left, hr, hl, total = lax.fori_loop(
            0, LANES // 8, local, (huge2, huge2, zero2, zero2, zero2)
        )
        total = 2.0 * total
        right, left = right + hr, left + hl
        fc, fs, f_all, fs_all = scan_all(right, total, 1, 8, inner, True)
        bc, bs, b_all, bs_all = scan_all(left, total, 1, 8, inner, False)
        gfc, gfs, gf_all, _ = scan_all(f_all, fs_all, 0, 4, outer, True)
        gbc, gbs, gb_all, _ = scan_all(b_all, bs_all, 0, 4, outer, False)
        first = jnp.full((8, LANES), core, jnp.int32) == 0
        xs[step, 0] = jnp.where(first, gf_all, gb_all)
        xs[step, 1] = jnp.broadcast_to(jnp.max(most, axis=0, keepdims=True), (8, LANES))
        copy = pltpu.make_async_remote_copy(
            src_ref=xs.at[step],
            dst_ref=xr.at[step],
            send_sem=sendx.at[step],
            recv_sem=recvx.at[step],
            device_id=(row, 1 - core),
            device_id_type=MESH,
        )
        copy.start()
        copy.wait()
        other = xr[step, 0]
        in_f = jnp.where(first, HUGE, other)
        in_b = jnp.where(first, other, HUGE)
        in_f = jnp.minimum(fc, jnp.minimum(gfc, in_f + gfs) + fs)
        in_b = jnp.minimum(bc, jnp.minimum(gbc, in_b + gbs) + bs)

        def final(b, carry):
            right, left, hr, hl = carry
            for s in range(8):
                i = b * 8 + s
                h = ht[at(i), :]
                right = jnp.minimum(xt[at(i), :], right + (hr + h))
                vf[at(i), :] = right
                hr = h
                h = ht[at(LANES - 1 - i), :]
                left = jnp.minimum(xt[at(LANES - 1 - i), :], left + (hl + h))
                vb[at(LANES - 1 - i), :] = left
                hl = h
            return (right, left, hr, hl)

        lax.fori_loop(0, LANES // 8, final, (in_f, in_b, zero2, zero2))

    most = vertical(0)
    horizontal(0, most)
    for j in range(8):
        rows = pl.ds(j, LANES, stride=8)
        back = jnp.minimum(vf[rows, :], vb[rows, :]).T
        x_ref[pl.ds((j // 4) * 16, 16), j % 4] = back.reshape(16, 8, LANES)
    most = vertical(1)
    horizontal(1, most)

    def merge(b, _):
        lines = pl.ds(pl.multiple_of(b * LANES, LANES), LANES)
        xt[lines, :] = jnp.minimum(vf[lines, :], vb[lines, :])
        return 0

    lax.fori_loop(0, 8, merge, 0)
    for j in range(8):
        back = xt[pl.ds(j, LANES, stride=8), :].T
        for r in range(16):
            i = (j // 4) * 16 + r
            lines = pl.ds(((i // 8) * 32 + (j % 4) * 8) * 8 + i % 8, 8, stride=8)
            on[lines, :] = back[r * 8 : (r + 1) * 8, :]
    out_cost = pltpu.make_async_copy(on, cost_hbm, out_sem.at[0])
    out_cost.start()

    for j in range(8):
        pair = jnp.minimum(xt[pl.ds(j, 64, stride=16), :], xt[pl.ds(j + 8, 64, stride=16), :])
        lines = jnp.concatenate([pair, pair], axis=0).T.reshape(8, 2, 8, LANES)
        pool[pl.ds((j // 4) * 8, 8), j % 4] = jnp.minimum(lines[:, 0], lines[:, 1])
        ht[pl.ds(j, 64, stride=8), :] = pair
    for a in range(16):
        for g in range(2):
            halves = [
                jnp.concatenate([pool[a, 2 * g + t, pl.ds(i, 4, stride=2), :] for t in range(2)], axis=0)
                for i in range(2)
            ]
            lines = pl.ds(((a // 8) * 16 + g * 8) * 8 + a % 8, 8, stride=8)
            o1[lines, :] = jnp.where(lane < 64, halves[0], halves[1])
    out_one = pltpu.make_async_copy(o1, one_hbm, out_sem.at[1])
    out_one.start()

    for j in range(8):
        quad = jnp.minimum(ht[pl.ds(j, 32, stride=16), :], ht[pl.ds(j + 8, 32, stride=16), :])
        lines = jnp.concatenate([quad] * 4, axis=0).T.reshape(4, 4, 8, LANES)
        lines = jnp.minimum(
            jnp.minimum(lines[:, 0], lines[:, 1]), jnp.minimum(lines[:, 2], lines[:, 3])
        )
        pool[pl.ds(16 + (j // 4) * 4, 4), j % 4] = lines
    for a in range(8):
        quarters = [
            jnp.concatenate([pool[16 + a, g, pl.ds(i, 2, stride=4), :] for g in range(4)], axis=0)
            for i in range(4)
        ]
        low = jnp.where(lane < 32, quarters[0], quarters[1])
        high = jnp.where(lane < 96, quarters[2], quarters[3])
        o2[pl.ds(a, 8, stride=8), :] = jnp.where(lane < 64, low, high)
    out_two = pltpu.make_async_copy(o2, two_hbm, out_sem.at[2])
    out_two.start()

    change_ref[0] = jnp.max(jnp.maximum(xs[1, 1], xr[1, 1]))
    out_cost.wait()
    out_one.wait()
    out_two.wait()


def lines_of(block):
    height, length = block.shape
    return (
        block.reshape(height // 8, 8, length // LANES, LANES)
        .transpose(0, 2, 1, 3)
        .reshape(-1, LANES)
    )


def block_of(lines, height):
    return (
        lines.reshape(height // 8, -1, 8, LANES).transpose(0, 2, 1, 3).reshape(height, -1)
    )


def shards(nz, np_, friction, sources):
    width = CHUNKS // np_
    f32 = jnp.float32
    anywhere = pl.BlockSpec(memory_space=pl.ANY)
    field = pltpu.VMEM((ROWS, 4, 8, LANES), f32)
    flat = pltpu.VMEM((ROWS * CHUNKS, LANES), f32)
    dma = pltpu.SemaphoreType.DMA
    cost, one, two, change = pl.pallas_call(
        functools.partial(kernel, nz, np_),
        out_shape=(
            jax.ShapeDtypeStruct((1024, LANES), f32),
            jax.ShapeDtypeStruct((256, LANES), f32),
            jax.ShapeDtypeStruct((64, LANES), f32),
            jax.ShapeDtypeStruct((1,), f32),
        ),
        in_specs=[anywhere, anywhere],
        out_specs=(anywhere, anywhere, anywhere, pl.BlockSpec(memory_space=pltpu.SMEM)),
        scratch_shapes=[
            flat,
            pltpu.VMEM((ROWS * CHUNKS, LANES), jnp.int32),
            field, field, field, field,
            flat, flat, flat, flat,
            flat,
            pltpu.VMEM((24, 4, 8, LANES), f32),
            pltpu.VMEM((256, LANES), f32),
            pltpu.VMEM((64, LANES), f32),
            pltpu.VMEM((np_, 3, width, LANES), f32),
            pltpu.VMEM((np_, 3, width, LANES), f32),
            pltpu.VMEM((nz, 3, width, LANES), f32),
            pltpu.VMEM((nz, 3, width, LANES), f32),
            pltpu.VMEM((np_, 5, width, LANES), f32),
            pltpu.VMEM((np_, 5, width, LANES), f32),
            pltpu.VMEM((nz, 5, width, LANES), f32),
            pltpu.VMEM((nz, 5, width, LANES), f32),
            pltpu.VMEM((2, np_, 3, width, LANES), f32),
            pltpu.VMEM((2, np_, 3, width, LANES), f32),
            pltpu.VMEM((np_, 4, width, LANES), f32),
            pltpu.VMEM((2, 4, 8, LANES), f32),
            pltpu.VMEM((2, 2, 8, LANES), f32),
            pltpu.VMEM((2, 2, 8, LANES), f32),
            dma((2,)),
            dma((3,)),
            dma((2, np_)), dma((2, np_)),
            dma((2, nz)), dma((2, nz)),
            dma((2, np_)), dma((2, np_)),
            dma((2,)), dma((2,)),
        ],
        compiler_params=pltpu.CompilerParams(collective_id=0, has_side_effects=True),
    )(lines_of(friction), lines_of(sources))
    return (block_of(cost, 32), block_of(one, 16), block_of(two, 8), change)


def solution(mesh):
    slabs = mesh.shape["rows"]
    plane = min(PLANE, slabs // 2)
    return jax.shard_map(
        functools.partial(shards, slabs // plane, plane),
        mesh=mesh,
        in_specs=(P("rows", "cols"), P("rows", "cols")),
        out_specs=(P("rows", "cols"), P("rows", "cols"), P("rows", "cols"), P()),
        check_vma=False,
    )
```

profile of v0, /device:TPU:1, one launch (start us, length us, event | category | flops | bytes accessed | tf_op | source)
XLA Modules:
  0.0 53.3 jit_solution(886236184563148671)
XLA Ops:
  0.6 47.7 %shard_map.57 = (f32[1024,128]{1,0:T(8,128)}, f32[256,128]{1,0:T(8,128)}, f32[64,128]{1,0:T(8,128)}, f32[1]{0:T(128)}) custom-call(f32[1024,128]{1,0:T(8,128)} %bitcast.25, s32[1024,128]{1,0:T(8,128)} %bitcast.26), custom_call_target="tpu_custom_call" | custom-call | tf_op jit(solution)/shard_map/pallas_call | solution.py:409
  48.3 0.0 copy-start
  48.3 1.9 %copy.10 = f32[32,4096]{1,0:T(8,128)} copy(f32[32,4096]{1,0:T(8,128)} %bitcast.27) | data formatting | bytes 1048576
  50.2 0.0 copy-done
  50.2 0.0 copy-start.1
  50.2 0.7 %copy.11 = f32[16,2048]{1,0:T(8,128)} copy(f32[16,2048]{1,0:T(8,128)S(1)} %bitcast.28) | data formatting | bytes 262144
  50.9 0.1 copy-done.1
  51.0 0.6 %copy.12 = f32[8,1024]{1,0:T(8,128)} copy(f32[8,1024]{1,0:T(8,128)S(1)} %bitcast.29) | data formatting | bytes 65536
Async XLA Ops:
  48.3 1.9 %copy-start = (f32[256,128]{1,0:T(8,128)S(1)}, f32[256,128]{1,0:T(8,128)}, u32[]{:S(2)}) copy-start(f32[256,128]{1,0:T(8,128)} %get-tuple-element.9) | copy-start | bytes 393220
  50.2 0.8 %copy-start.1 = (f32[64,128]{1,0:T(8,128)S(1)}, f32[64,128]{1,0:T(8,128)}, u32[]{:S(2)}) copy-start(f32[64,128]{1,0:T(8,128)} %get-tuple-element.10) | copy-start | bytes 98308
where the time goes:
time: 53.5 us; the launch traced here: 53.3 us
  Pallas kernels  47.7 us (89%)
  local copies, waits for them, and re-layouts  3.28 us (6%)
  between operations  2.4 us (4%)
    pallas_call x1, Pallas kernels, shards(): pl.pallas_call(functools.partial(kernel, nz, np_), out_shape=(jax.ShapeDt...  47.7 us
    unnamed x7, local copies, waits for them, and re-layouts  3.28 us

commit v1 on v0

v1 whole, which is shorter than its diff:
```python
import functools

import jax
import jax.numpy as jnp
from jax import lax
from jax.experimental import pallas as pl
from jax.experimental.pallas import tpu as pltpu
from jax.sharding import PartitionSpec as P

HUGE = 1e30
MESH = pl.DeviceIdType.MESH
ROWS = 32
CHUNKS = 32
LANES = 128
PLANE = (4, 4)
HUB = 1
PARTS = 4
STEPS = LANES // PARTS


def far_first(sizes):
    offsets = [()]
    for size in sizes:
        offsets = [(*o, k) for o in offsets for k in range(size)]
    hops = lambda o: sum(min(k, s - k) for k, s in zip(o, sizes))
    return sorted((o for o in offsets if any(o)), key=hops, reverse=True)


def kernel(
    nz, plane, f_hbm, s_hbm, lines_ref, change_ref,
    fn, sn, h_ref, x_ref, d_ref, u_ref, ht, xt, vf, vb,
    s1a, r1a, s2a, r2a, s1b, r1b, s2b, r2b, s3, r3, pre, enter, xs, xr, paths,
    in_sem, send1, recv1, send2, recv2, send3, recv3, sendx, recvx,
):
    px, py = plane
    np_ = px * py
    width = CHUNKS // np_
    row = lax.axis_index("rows")
    core = lax.axis_index("cols")
    z, p = row // np_, row % np_
    x, y = p // py, p % py
    other_core = 1 - core
    hub = core == HUB
    tile = (4, 8, LANES)
    part = (2, width, LANES)
    near_plane = far_first(plane)
    near_z = far_first((nz,))

    def in_copies(b):
        lines = pl.ds(pl.multiple_of(b * 256, 256), 256)
        return (
            pltpu.make_async_copy(f_hbm.at[lines], fn.at[lines], in_sem.at[0, b]),
            pltpu.make_async_copy(s_hbm.at[lines], sn.at[lines], in_sem.at[1, b]),
        )

    for b in range(4):
        for copy in in_copies(b):
            copy.start()

    def slot(k):
        dx, dy = near_plane[k]
        return ((x + dx) % px) * py + (y + dy) % py

    def z_slot(k):
        return (z + near_z[k][0]) % nz

    barrier = pltpu.get_barrier_semaphore()

    def greet(device):
        pl.semaphore_signal(barrier, inc=1, device_id=device, device_id_type=MESH)

    for k in range(np_ - 1):
        greet((z * np_ + slot(k), HUB))

    @pl.when(hub)
    def _():
        for k in range(np_ - 1):
            greet((z * np_ + slot(k), 1 - HUB))
        for k in range(nz - 1):
            greet((z_slot(k) * np_ + p, HUB))

    greet((row, other_core))

    def wait_for_peers():
        @pl.when(hub)
        def _():
            pl.semaphore_wait(barrier, 2 * (np_ - 1) + nz)

        @pl.when(jnp.logical_not(hub))
        def _():
            pl.semaphore_wait(barrier, np_)

    huge = jnp.full(tile, HUGE, jnp.float32)
    zero = jnp.zeros(tile, jnp.float32)

    def spread(b, _):
        for copy in in_copies(b):
            copy.wait()
        for s in range(8):
            for g in range(4):
                lines = pl.ds((b * 32 + g * 8) * 8 + s, 8, stride=8)
                h_ref[b * 8 + s, g] = 0.5 * fn[lines, :]
                x_ref[b * 8 + s, g] = jnp.where(sn[lines, :] == 1, 0.0, HUGE)
        return 0

    lax.fori_loop(0, ROWS // 8, spread, 0)

    def first_local(b, carry):
        down, up, hd, hu, total = carry
        for s in range(8):
            i = b * 8 + s
            h = h_ref[i]
            down = jnp.minimum(x_ref[i], down + (hd + h))
            total = total + h
            hd = h
            h = h_ref[ROWS - 1 - i]
            up = jnp.minimum(x_ref[ROWS - 1 - i], up + (hu + h))
            hu = h
        return (down, up, hd, hu, total)

    def second_local(b, carry):
        down, up, hd, hu, far_d, far_u, most = carry
        for s in range(8):
            i = b * 8 + s
            h, v = h_ref[i], x_ref[i]
            down = jnp.minimum(v, down + (hd + h))
            far_d = jnp.maximum(v, far_d - (hd + h))
            most = jnp.maximum(most, v - down)
            hd = h
            h, v = h_ref[ROWS - 1 - i], x_ref[ROWS - 1 - i]
            up = jnp.minimum(v, up + (hu + h))
            far_u = jnp.maximum(v, far_u - (hu + h))
            most = jnp.maximum(most, v - up)
            hu = h
        return (down, up, hd, hu, far_d, far_u, most)

    def put(to, item, value):
        for q in range(np_):
            line = q * width
            to[q, item] = value[line // 8, line % 8 : line % 8 + width, :]

    def remote(src, dst, send, recv, device):
        return pltpu.make_async_remote_copy(
            src_ref=src, dst_ref=dst, send_sem=send, recv_sem=recv,
            device_id=device, device_id_type=MESH,
        )

    my_z = jnp.full(part, z, jnp.int32)

    def pick(k, new, old):
        return jnp.where(my_z == k, new, old)

    def vertical(step, window):
        s1, r1, s2, r2 = ((s1a, r1a, s2a, r2a), (s1b, r1b, s2b, r2b))[step]
        if step == 0:
            down, up, hd, hu, total = lax.fori_loop(
                0, ROWS // 8, first_local, (huge, huge, zero, zero, zero)
            )
            values = (up + hu, down + hd, 2.0 * total)
        else:
            down, up, hd, hu, far_d, far_u, most = lax.fori_loop(
                0, ROWS // 8, second_local, (huge, huge, zero, zero, -huge, -huge, zero)
            )
            values = (up + hu, down + hd, far_u - hu, far_d - hd, most)
        items = len(values)
        for item, value in enumerate(values):
            put(s1, item, value)
        if step == 0:
            wait_for_peers()
        copies = []
        for k in range(np_ - 1):
            copy = remote(
                s1.at[slot(k)], r1.at[p, :, core], send1.at[step, k], recv1.at[step, core, k],
                (z * np_ + slot(k), HUB),
            )
            copy.start()
            copies.append(copy)
        last = np_ - 1
        to_hub = remote(
            s1.at[p], r1.at[p, :, core], send1.at[step, last], recv1.at[step, core, last], (row, HUB)
        )

        @pl.when(jnp.logical_not(hub))
        def _():
            to_hub.start()

        window()

        for copy in copies:
            copy.wait_send()

        @pl.when(jnp.logical_not(hub))
        def _():
            to_hub.wait_send()

        to, got = s3.at[step], r3.at[step]

        @pl.when(hub)
        def _():
            for item in range(items):
                r1[p, item, HUB] = s1[p, item]
            for k in range(np_):
                for half in range(2):
                    if k == last and half == HUB:
                        continue
                    remote(
                        s1.at[p], r1.at[p, :, half], send1.at[step, k], recv1.at[step, half, k], (row, HUB)
                    ).wait_recv()
            near = jnp.full(part, HUGE, jnp.float32)
            none = jnp.zeros(part, jnp.float32)
            b, a, s_down, s_up, far_d, far_u, most = near, near, none, none, -near, -near, none
            for q in range(np_):
                r_a, r_b = r1[q, 0], r1[q, 1]
                if step == 0:
                    s = r1[q, 2]
                    pre[q, 2] = s_down
                    s_down = s_down + s
                else:
                    s = r1a[q, 2]
                    most = jnp.maximum(most, jnp.maximum(far_d - r_a, r1[q, 2] - b))
                    most = jnp.maximum(most, r1[q, 4])
                    far_d = jnp.maximum(r1[q, 3], far_d - s)
                pre[q, 0] = b
                b = jnp.minimum(r_b, b + s)
            for q in range(np_ - 1, -1, -1):
                s = r1a[q, 2]
                if step == 0:
                    pre[q, 3] = s_up
                    s_up = s_up + s
                else:
                    far_u = jnp.maximum(r1[q, 2], far_u - s)
                pre[q, 1] = a
                a = jnp.minimum(r1[q, 0], a + s)
            values = (a, b, s_down) if step == 0 else (a, b, far_u, far_d, most)
            for item, value in enumerate(values):
                s2[item] = value
            copies = []
            for k in range(nz - 1):
                copy = remote(
                    s2, r2.at[z], send2.at[step, k], recv2.at[step, k], (z_slot(k) * np_ + p, HUB)
                )
                copy.start()
                copies.append(copy)
            for item in range(items):
                r2[z, item] = values[item]
            for copy in copies:
                copy.wait()

            b, a, far_d, most = near, near, -near, none
            in_d, in_u = near, near
            for k in range(nz):
                in_d = pick(k, b, in_d)
                s = r2a[k, 2]
                if step == 1:
                    most = jnp.maximum(most, jnp.maximum(far_d - r2[k, 0], r2[k, 2] - b))
                    most = jnp.maximum(most, r2[k, 4])
                    far_d = jnp.maximum(r2[k, 3], far_d - s)
                b = jnp.minimum(r2[k, 1], b + s)
            for k in range(nz - 1, -1, -1):
                in_u = pick(k, a, in_u)
                a = jnp.minimum(r2[k, 0], a + r2a[k, 2])
            most = jnp.maximum(most[0], most[1])
            for q in range(np_):
                to[q, 0] = jnp.minimum(pre[q, 0], in_d + pre[q, 2])
                to[q, 1] = jnp.minimum(pre[q, 1], in_u + pre[q, 3])
                to[q, 2, 0] = most
                to[q, 2, 1] = most
            copies = []
            for k in range(np_):
                for half in range(2):
                    if k == last and half == HUB:
                        continue
                    q = p if k == last else slot(k)
                    copy = remote(
                        to.at[q, :, half], got.at[p], send3.at[step, half, k], recv3.at[step, k],
                        (z * np_ + q, half),
                    )
                    copy.start()
                    copies.append(copy)
            for item in range(3):
                got[p, item] = to[p, item, HUB]
            for copy in copies:
                copy.wait_send()

        def from_hub(k):
            return remote(
                to.at[p, :, 0], got.at[p], send3.at[step, 0, k], recv3.at[step, k], (row, HUB)
            )

        for k in range(last):
            from_hub(k).wait_recv()

        @pl.when(jnp.logical_not(hub))
        def _():
            from_hub(last).wait_recv()

        most = got[0, 2]
        for q in range(np_):
            line = q * width
            for item in range(2):
                enter[item, line // 8, line % 8 : line % 8 + width, :] = got[q, item]
            most = jnp.maximum(most, got[q, 2])

        def final(b, carry):
            down, up, hd, hu = carry
            for s in range(8):
                i = b * 8 + s
                h = h_ref[i]
                down = jnp.minimum(x_ref[i], down + (hd + h))
                d_ref[i] = down
                hd = h
                h = h_ref[ROWS - 1 - i]
                up = jnp.minimum(x_ref[ROWS - 1 - i], up + (hu + h))
                u_ref[ROWS - 1 - i] = up
                hu = h
            return (down, up, hd, hu)

        lax.fori_loop(0, ROWS // 8, final, (enter[0], enter[1], zero, zero))
        return most

    lane = lax.broadcasted_iota(jnp.int32, (8, LANES), 1)
    sub = lax.broadcasted_iota(jnp.int32, (8, LANES), 0)
    inner, outer = lane % 8, sub % 4
    huge2 = jnp.full((8, LANES), HUGE, jnp.float32)
    zero2 = jnp.zeros((8, LANES), jnp.float32)

    def block(load, j):
        return load(pl.ds((j // 4) * 16, 16), j % 4).reshape(LANES, LANES)

    def at(i):
        return pl.ds(pl.multiple_of(i * 8, 8), 8)

    def chunk_path(shift):
        return paths[11 + shift]

    def group_path(shift):
        return paths[22 + shift]

    def measure():
        for j in range(8):
            ht[pl.ds(j, LANES, stride=8), :] = block(lambda r, g: h_ref[r, g], j).T

        def add(b, sums):
            return tuple(
                sum((ht[at(k * STEPS + b * 8 + s), :] for s in range(8)), start=sums[k])
                for k in range(PARTS)
            )

        sums = lax.fori_loop(0, STEPS // 8, add, (zero2,) * PARTS)
        for k in range(PARTS):
            paths[k] = 2.0 * sums[k]
        whole = 2.0 * (sums[0] + sums[1] + sums[2] + sums[3])
        before = after = zero2
        for k in range(-7, 8):
            rolled = pltpu.roll(whole, k % LANES, 1)
            paths[11 + k] = rolled
            if k > 0:
                before = jnp.where(inner >= k, before + rolled, before)
            if k < 0:
                after = jnp.where(inner - k < 8, after + rolled, after)
        paths[26] = before
        paths[27] = after
        whole = before + whole + after
        before = after = zero2
        for k in range(-3, 4):
            rolled = pltpu.roll(whole, k % 8, 0)
            paths[22 + k] = rolled
            if k > 0:
                before = jnp.where(outer >= k, before + rolled, before)
            if k < 0:
                after = jnp.where(outer - k < 4, after + rolled, after)
        paths[28] = before
        paths[29] = after

    def scan_all(c, path, axis, size, place, forward):
        step = 1 if forward else -1
        extent = c.shape[axis]
        at_place = place if forward else size - 1 - place
        run = huge2
        for k in range(size - 1, 0, -1):
            ck = pltpu.roll(c, (step * k) % extent, axis)
            run = jnp.where(at_place >= k, jnp.minimum(ck, run + path(step * k)), run)
        before = run
        run = jnp.minimum(c, run + path(0))
        for k in range(1, size):
            ck = pltpu.roll(c, (-step * k) % extent, axis)
            run = jnp.where(at_place + k < size, jnp.minimum(ck, run + path(-step * k)), run)
        return before, run

    def horizontal(step):
        for j in range(8):
            rows = pl.ds(j, LANES, stride=8)
            xt[rows, :] = block(lambda r, g: jnp.minimum(d_ref[r, g], u_ref[r, g]), j).T

        def sweep(start_f, start_b, store):
            def some(b, carry):
                right, left, hr, hl = (list(c) for c in carry)
                for s in range(8):
                    for k in range(PARTS):
                        i = k * STEPS + b * 8 + s
                        h = ht[at(i), :]
                        right[k] = jnp.minimum(xt[at(i), :], right[k] + (hr[k] + h))
                        if store:
                            vf[at(i), :] = right[k]
                        hr[k] = h
                        i = (k + 1) * STEPS - 1 - (b * 8 + s)
                        h = ht[at(i), :]
                        left[k] = jnp.minimum(xt[at(i), :], left[k] + (hl[k] + h))
                        if store:
                            vb[at(i), :] = left[k]
                        hl[k] = h
                return (tuple(right), tuple(left), tuple(hr), tuple(hl))

            zeros = (zero2,) * PARTS
            return lax.fori_loop(0, STEPS // 8, some, (start_f, start_b, zeros, zeros))

        right, left, hr, hl = sweep((huge2,) * PARTS, (huge2,) * PARTS, False)
        right = [r + h for r, h in zip(right, hr)]
        left = [r + h for r, h in zip(left, hl)]
        c_f, c_b = right[0], left[-1]
        for k in range(1, PARTS):
            c_f = jnp.minimum(right[k], c_f + paths[k])
            c_b = jnp.minimum(left[-1 - k], c_b + paths[PARTS - 1 - k])
        fc, f_all = scan_all(c_f, chunk_path, 1, 8, inner, True)
        bc, b_all = scan_all(c_b, chunk_path, 1, 8, inner, False)
        gfc, gf_all = scan_all(f_all, group_path, 0, 4, outer, True)
        gbc, gb_all = scan_all(b_all, group_path, 0, 4, outer, False)
        first = jnp.full((8, LANES), core, jnp.int32) == 0
        xs[step] = jnp.where(first, gf_all, gb_all)
        copy = remote(xs.at[step], xr.at[step], sendx.at[step], recvx.at[step], (row, other_core))
        copy.start()
        copy.wait()
        other = xr[step]
        in_f = jnp.where(first, HUGE, other)
        in_b = jnp.where(first, other, HUGE)
        in_f = [jnp.minimum(fc, jnp.minimum(gfc, in_f + paths[28]) + paths[26])]
        in_b = [jnp.minimum(bc, jnp.minimum(gbc, in_b + paths[29]) + paths[27])]
        for k in range(PARTS - 1):
            in_f.append(jnp.minimum(right[k], in_f[k] + paths[k]))
            in_b.append(jnp.minimum(left[-1 - k], in_b[k] + paths[PARTS - 1 - k]))
        sweep(tuple(in_f), tuple(in_b[::-1]), True)

    vertical(0, measure)
    horizontal(0)
    for j in range(8):
        rows = pl.ds(j, LANES, stride=8)
        back = jnp.minimum(vf[rows, :], vb[rows, :]).T
        x_ref[pl.ds((j // 4) * 16, 16), j % 4] = back.reshape(16, 8, LANES)
    most = vertical(1, lambda: None)
    horizontal(1)
    change_ref[0] = jnp.max(most)

    def merge(b, _):
        lines = pl.ds(pl.multiple_of(b * LANES, LANES), LANES)
        lines_ref[lines, :] = jnp.minimum(vf[lines, :], vb[lines, :])
        return 0

    lax.fori_loop(0, 8, merge, 0)


def finish(xt, most, cost_hbm, one_hbm, two_hbm, change_ref, on, pairs, pool, o1, o2, out_sem):
    lane = lax.broadcasted_iota(jnp.int32, (8, LANES), 1)
    for j in range(8):
        back = xt[pl.ds(j, LANES, stride=8), :].T
        for r in range(16):
            i = (j // 4) * 16 + r
            lines = pl.ds(((i // 8) * 32 + (j % 4) * 8) * 8 + i % 8, 8, stride=8)
            on[lines, :] = back[r * 8 : (r + 1) * 8, :]
    out_cost = pltpu.make_async_copy(on, cost_hbm, out_sem.at[0])
    out_cost.start()

    for j in range(8):
        pair = jnp.minimum(xt[pl.ds(j, 64, stride=16), :], xt[pl.ds(j + 8, 64, stride=16), :])
        lines = jnp.concatenate([pair, pair], axis=0).T.reshape(8, 2, 8, LANES)
        pool[pl.ds((j // 4) * 8, 8), j % 4] = jnp.minimum(lines[:, 0], lines[:, 1])
        pairs[pl.ds(j, 64, stride=8), :] = pair
    for a in range(16):
        for g in range(2):
            halves = [
                jnp.concatenate([pool[a, 2 * g + t, pl.ds(i, 4, stride=2), :] for t in range(2)], axis=0)
                for i in range(2)
            ]
            lines = pl.ds(((a // 8) * 16 + g * 8) * 8 + a % 8, 8, stride=8)
            o1[lines, :] = jnp.where(lane < 64, halves[0], halves[1])
    out_one = pltpu.make_async_copy(o1, one_hbm, out_sem.at[1])
    out_one.start()

    for j in range(8):
        quad = jnp.minimum(pairs[pl.ds(j, 32, stride=16), :], pairs[pl.ds(j + 8, 32, stride=16), :])
        lines = jnp.concatenate([quad] * 4, axis=0).T.reshape(4, 4, 8, LANES)
        lines = jnp.minimum(
            jnp.minimum(lines[:, 0], lines[:, 1]), jnp.minimum(lines[:, 2], lines[:, 3])
        )
        pool[pl.ds(16 + (j // 4) * 4, 4), j % 4] = lines
    for a in range(8):
        quarters = [
            jnp.concatenate([pool[16 + a, g, pl.ds(i, 2, stride=4), :] for g in range(4)], axis=0)
            for i in range(4)
        ]
        low = jnp.where(lane < 32, quarters[0], quarters[1])
        high = jnp.where(lane < 96, quarters[2], quarters[3])
        o2[pl.ds(a, 8, stride=8), :] = jnp.where(lane < 64, low, high)
    out_two = pltpu.make_async_copy(o2, two_hbm, out_sem.at[2])
    out_two.start()
    change_ref[0] = most[0]
    out_cost.wait()
    out_one.wait()
    out_two.wait()


def lines_of(block):
    height, length = block.shape
    return (
        block.reshape(height // 8, 8, length // LANES, LANES)
        .transpose(0, 2, 1, 3)
        .reshape(-1, LANES)
    )


def block_of(lines, height):
    return lines.reshape(height // 8, -1, 8, LANES).transpose(0, 2, 1, 3).reshape(height, -1)


def shards(nz, plane, friction, sources):
    np_ = plane[0] * plane[1]
    width = CHUNKS // np_
    f32 = jnp.float32
    anywhere = pl.BlockSpec(memory_space=pltpu.HBM)
    in_vmem = pl.BlockSpec(memory_space=pltpu.VMEM)
    in_smem = pl.BlockSpec(memory_space=pltpu.SMEM)
    field = pltpu.VMEM((ROWS, 4, 8, LANES), f32)
    flat = pltpu.VMEM((ROWS * CHUNKS, LANES), f32)
    dma = pltpu.SemaphoreType.DMA

    def message(count, items, *halves):
        return pltpu.VMEM((*count, items, *halves, width, LANES), f32)

    def in_hbm(block):
        return pltpu.with_memory_space_constraint(lines_of(block), pltpu.HBM)

    rounds = []
    for items in (3, 5):
        rounds += [message((np_,), items), message((np_,), items, 2), message((), items, 2), message((nz,), items, 2)]
    lines, change = pl.pallas_call(
        functools.partial(kernel, nz, plane),
        out_shape=(jax.ShapeDtypeStruct((1024, LANES), f32), jax.ShapeDtypeStruct((1,), f32)),
        in_specs=[anywhere, anywhere],
        out_specs=(in_vmem, in_smem),
        scratch_shapes=[
            flat,
            pltpu.VMEM((ROWS * CHUNKS, LANES), jnp.int32),
            field, field, field, field,
            flat, flat, flat, flat,
            *rounds,
            message((2, np_), 3, 2),
            message((2, np_), 3),
            message((np_,), 4, 2),
            pltpu.VMEM((2, 4, 8, LANES), f32),
            pltpu.VMEM((2, 8, LANES), f32),
            pltpu.VMEM((2, 8, LANES), f32),
            pltpu.VMEM((30, 8, LANES), f32),
            dma((2, 4)),
            dma((2, np_)), dma((2, 2, np_)),
            dma((2, nz)), dma((2, nz)),
            dma((2, 2, np_)), dma((2, np_)),
            dma((2,)), dma((2,)),
        ],
        compiler_params=pltpu.CompilerParams(
            collective_id=0, has_side_effects=True, vmem_limit_bytes=16 * 1024 * 1024
        ),
    )(in_hbm(friction), in_hbm(sources))
    cost, one, two, change = pl.pallas_call(
        finish,
        out_shape=(
            jax.ShapeDtypeStruct((1024, LANES), f32),
            jax.ShapeDtypeStruct((256, LANES), f32),
            jax.ShapeDtypeStruct((64, LANES), f32),
            jax.ShapeDtypeStruct((1,), f32),
        ),
        in_specs=[in_vmem, in_smem],
        out_specs=(anywhere, anywhere, anywhere, in_smem),
        scratch_shapes=[
            flat,
            pltpu.VMEM((512, LANES), f32),
            pltpu.VMEM((24, 4, 8, LANES), f32),
            pltpu.VMEM((256, LANES), f32),
            pltpu.VMEM((64, LANES), f32),
            dma((3,)),
        ],
        compiler_params=pltpu.CompilerParams(vmem_limit_bytes=16 * 1024 * 1024),
    )(lines, change)
    return (block_of(cost, 32), block_of(one, 16), block_of(two, 8), change)


def solution(mesh):
    slabs = mesh.shape["rows"]
    plane = PLANE if slabs >= 32 else (2, 2)
    return jax.shard_map(
        functools.partial(shards, slabs // (plane[0] * plane[1]), plane),
        mesh=mesh,
        in_specs=(P("rows", "cols"), P("rows", "cols")),
        out_specs=(P("rows", "cols"), P("rows", "cols"), P("rows", "cols"), P()),
        check_vma=False,
    )
```

time: 53.5 us -> 45.1 us (0.84)
  Pallas kernels: 47.7 us -> 44.4 us
  local copies, waits for them, and re-layouts: 3.28 us -> 0 us
  between operations: 2.4 us -> 0.64 us
    unnamed x7 -> x0, local copies, waits for them, and re-layouts: 3.28 us -> none
    pallas_call x1 -> x2, Pallas kernels: 47.7 us -> 44.4 us  [the longest x1 41.9 us: shards(): pl.pallas_call(functools.partial(kernel, nz, plane), out_shape=(jax.Shape...]
where the time goes in v1:
time: 45.1 us; the launch traced here: 45 us
  Pallas kernels  44.4 us (98%)
  between operations  0.64 us (1%)
    pallas_call x1, Pallas kernels, shards(): pl.pallas_call(functools.partial(kernel, nz, plane), out_shape=(jax.Shape...  41.9 us
    pallas_call x1, Pallas kernels, shards(): pl.pallas_call(finish, out_shape=(jax.ShapeDtypeStruct((1024, LANES), f32...  2.44 us

profile of v1, /device:TPU:1, one launch (start us, length us, event | category | flops | bytes accessed | tf_op | source)
XLA Modules:
  0.0 45.0 jit_solution(7449082541249852676)
XLA Ops:
  0.6 41.9 %shard_map.57 = (f32[1024,128]{1,0:T(8,128)S(1)}, f32[1]{0:T(128)}) custom-call(f32[1024,128]{1,0:T(8,128)} %bitcast.25, s32[1024,128]{1,0:T(8,128)} %bitcast.26), custom_call_target="tpu_custom_call" | custom-call | tf_op jit(solution)/shard_map/pallas_call | solution.py:544
  42.6 2.4 %shard_map.58 = (f32[1024,128]{1,0:T(8,128)}, f32[256,128]{1,0:T(8,128)}, f32[64,128]{1,0:T(8,128)}, f32[1]{0:T(128)}) custom-call(f32[1024,128]{1,0:T(8,128)S(1)} %get-tuple-element.10.xt, f32[1]{0:T(128)} %get-tuple-element.11.most), custom_call_target="tpu_custom_call" | custom-call | tf_op jit(solution)/shard_map/pallas_call | solution.py:572

commit v2 on v1

--- a/solution.py
+++ b/solution.py
@@ -28,7 +28,7 @@
 
 def kernel(
     nz, plane, f_hbm, s_hbm, lines_ref, change_ref,
-    fn, sn, h_ref, x_ref, d_ref, u_ref, ht, xt, vf, vb,
+    fn, sn, h_ref, x_ref, d_ref, u_ref, ht, xt, vf, vb, edge,
     s1a, r1a, s2a, r2a, s1b, r1b, s2b, r2b, s3, r3, pre, enter, xs, xr, paths,
     in_sem, send1, recv1, send2, recv2, send3, recv3, sendx, recvx,
 ):
@@ -37,8 +37,8 @@
     width = CHUNKS // np_
     row = lax.axis_index("rows")
     core = lax.axis_index("cols")
-    z, p = row // np_, row % np_
-    x, y = p // py, p % py
+    z, p = lax.div(row, np_), lax.rem(row, np_)
+    x, y = lax.div(p, py), lax.rem(p, py)
     other_core = 1 - core
     hub = core == HUB
     tile = (4, 8, LANES)
@@ -53,16 +53,12 @@
             pltpu.make_async_copy(s_hbm.at[lines], sn.at[lines], in_sem.at[1, b]),
         )
 
-    for b in range(4):
-        for copy in in_copies(b):
-            copy.start()
-
     def slot(k):
         dx, dy = near_plane[k]
-        return ((x + dx) % px) * py + (y + dy) % py
+        return lax.rem(x + dx, px) * py + lax.rem(y + dy, py)
 
     def z_slot(k):
-        return (z + near_z[k][0]) % nz
+        return lax.rem(z + near_z[k][0], nz)
 
     barrier = pltpu.get_barrier_semaphore()
 
@@ -80,6 +76,10 @@
             greet((z_slot(k) * np_ + p, HUB))
 
     greet((row, other_core))
+
+    for b in range(4):
+        for copy in in_copies(b):
+            copy.start()
 
     def wait_for_peers():
         @pl.when(hub)
@@ -266,8 +266,8 @@
                 to[q, 2, 0] = most
                 to[q, 2, 1] = most
             copies = []
-            for k in range(np_):
-                for half in range(2):
+            for half in (1 - HUB, HUB):
+                for k in range(np_):
                     if k == last and half == HUB:
                         continue
                     q = p if k == last else slot(k)
@@ -372,6 +372,17 @@
         paths[28] = before
         paths[29] = after
 
+        def border(i, path):
+            i = core * i + other_core * (LANES - 1 - i)
+            h = ht[at(i), :]
+            edge[at(i), :] = path + h
+            return path + 2.0 * h
+
+        first = jnp.full((8, LANES), core, jnp.int32) == 0
+        lax.fori_loop(
+            0, LANES, border, jnp.where(first, paths[27] + paths[29], paths[26] + paths[28])
+        )
+
     def scan_all(c, path, axis, size, place, forward):
         step = 1 if forward else -1
         extent = c.shape[axis]
@@ -387,7 +398,7 @@
             run = jnp.where(at_place + k < size, jnp.minimum(ck, run + path(-step * k)), run)
         return before, run
 
-    def horizontal(step):
+    def horizontal(step, window):
         for j in range(8):
             rows = pl.ds(j, LANES, stride=8)
             xt[rows, :] = block(lambda r, g: jnp.minimum(d_ref[r, g], u_ref[r, g]), j).T
@@ -429,30 +440,36 @@
         xs[step] = jnp.where(first, gf_all, gb_all)
         copy = remote(xs.at[step], xr.at[step], sendx.at[step], recvx.at[step], (row, other_core))
         copy.start()
-        copy.wait()
-        other = xr[step]
-        in_f = jnp.where(first, HUGE, other)
-        in_b = jnp.where(first, other, HUGE)
-        in_f = [jnp.minimum(fc, jnp.minimum(gfc, in_f + paths[28]) + paths[26])]
-        in_b = [jnp.minimum(bc, jnp.minimum(gbc, in_b + paths[29]) + paths[27])]
+        in_f = [jnp.minimum(fc, gfc + paths[26])]
+        in_b = [jnp.minimum(bc, gbc + paths[27])]
         for k in range(PARTS - 1):
             in_f.append(jnp.minimum(right[k], in_f[k] + paths[k]))
             in_b.append(jnp.minimum(left[-1 - k], in_b[k] + paths[PARTS - 1 - k]))
         sweep(tuple(in_f), tuple(in_b[::-1]), True)
+        window()
+        copy.wait()
+        return xr[step]
+
+    def in_row(other, j):
+        rows = pl.ds(j, LANES, stride=8)
+        return jnp.minimum(jnp.minimum(vf[rows, :], vb[rows, :]), edge[rows, :] + other[j : j + 1])
 
     vertical(0, measure)
-    horizontal(0)
+    other = horizontal(0, lambda: None)
     for j in range(8):
-        rows = pl.ds(j, LANES, stride=8)
-        back = jnp.minimum(vf[rows, :], vb[rows, :]).T
+        back = in_row(other, j).T
         x_ref[pl.ds((j // 4) * 16, 16), j % 4] = back.reshape(16, 8, LANES)
     most = vertical(1, lambda: None)
-    horizontal(1)
-    change_ref[0] = jnp.max(most)
+
+    def reduce_change():
+        change_ref[0] = jnp.max(most)
+
+    other = horizontal(1, reduce_change)
 
     def merge(b, _):
-        lines = pl.ds(pl.multiple_of(b * LANES, LANES), LANES)
-        lines_ref[lines, :] = jnp.minimum(vf[lines, :], vb[lines, :])
+        for t in range(16):
+            i = at(b * 16 + t)
+            lines_ref[i, :] = jnp.minimum(jnp.minimum(vf[i, :], vb[i, :]), edge[i, :] + other)
         return 0
 
     lax.fori_loop(0, 8, merge, 0)
@@ -460,14 +477,17 @@
 
 def finish(xt, most, cost_hbm, one_hbm, two_hbm, change_ref, on, pairs, pool, o1, o2, out_sem):
     lane = lax.broadcasted_iota(jnp.int32, (8, LANES), 1)
+    outs = []
     for j in range(8):
         back = xt[pl.ds(j, LANES, stride=8), :].T
         for r in range(16):
             i = (j // 4) * 16 + r
             lines = pl.ds(((i // 8) * 32 + (j % 4) * 8) * 8 + i % 8, 8, stride=8)
             on[lines, :] = back[r * 8 : (r + 1) * 8, :]
-    out_cost = pltpu.make_async_copy(on, cost_hbm, out_sem.at[0])
-    out_cost.start()
+        if j % 4 == 3:
+            half = pl.ds((j // 4) * 512, 512)
+            outs.append(pltpu.make_async_copy(on.at[half], cost_hbm.at[half], out_sem.at[2 + j // 4]))
+            outs[-1].start()
 
     for j in range(8):
         pair = jnp.minimum(xt[pl.ds(j, 64, stride=16), :], xt[pl.ds(j + 8, 64, stride=16), :])
@@ -482,7 +502,7 @@
             ]
             lines = pl.ds(((a // 8) * 16 + g * 8) * 8 + a % 8, 8, stride=8)
             o1[lines, :] = jnp.where(lane < 64, halves[0], halves[1])
-    out_one = pltpu.make_async_copy(o1, one_hbm, out_sem.at[1])
+    out_one = pltpu.make_async_copy(o1, one_hbm, out_sem.at[0])
     out_one.start()
 
     for j in range(8):
@@ -500,10 +520,11 @@
         low = jnp.where(lane < 32, quarters[0], quarters[1])
         high = jnp.where(lane < 96, quarters[2], quarters[3])
         o2[pl.ds(a, 8, stride=8), :] = jnp.where(lane < 64, low, high)
-    out_two = pltpu.make_async_copy(o2, two_hbm, out_sem.at[2])
+    out_two = pltpu.make_async_copy(o2, two_hbm, out_sem.at[1])
     out_two.start()
     change_ref[0] = most[0]
-    out_cost.wait()
+    for out in outs:
+        out.wait()
     out_one.wait()
     out_two.wait()
 
@@ -550,7 +571,7 @@
             flat,
             pltpu.VMEM((ROWS * CHUNKS, LANES), jnp.int32),
             field, field, field, field,
-            flat, flat, flat, flat,
+            flat, flat, flat, flat, flat,
             *rounds,
             message((2, np_), 3, 2),
             message((2, np_), 3),
@@ -585,7 +606,7 @@
             pltpu.VMEM((24, 4, 8, LANES), f32),
             pltpu.VMEM((256, LANES), f32),
             pltpu.VMEM((64, LANES), f32),
-            dma((3,)),
+            dma((4,)),
         ],
         compiler_params=pltpu.CompilerParams(vmem_limit_bytes=16 * 1024 * 1024),
     )(lines, change)

time: 45.1 us -> 44.5 us (0.987)
  Pallas kernels: 44.4 us -> 43.8 us
    pallas_call x1, Pallas kernels: 41.9 us -> 41.3 us  [shards(): pl.pallas_call(functools.partial(kernel, nz, plane), out_shape=(jax.Shape...]
where the time goes in v2:
time: 44.5 us; the launch traced here: 44.4 us
  Pallas kernels  43.8 us (98%)
  between operations  0.64 us (1%)
    pallas_call x1, Pallas kernels, shards(): pl.pallas_call(functools.partial(kernel, nz, plane), out_shape=(jax.Shape...  41.3 us
    pallas_call x1, Pallas kernels, shards(): pl.pallas_call(finish, out_shape=(jax.ShapeDtypeStruct((1024, LANES), f32...  2.46 us

profile of v2, /device:TPU:1, one launch (start us, length us, event | category | flops | bytes accessed | tf_op | source)
XLA Modules:
  0.0 44.4 jit_solution(17007960927177976906)
XLA Ops:
  0.6 41.3 %shard_map.57 = (f32[1024,128]{1,0:T(8,128)S(1)}, f32[1]{0:T(128)}) custom-call(f32[1024,128]{1,0:T(8,128)} %bitcast.25, s32[1024,128]{1,0:T(8,128)} %bitcast.26), custom_call_target="tpu_custom_call" | custom-call | tf_op jit(solution)/shard_map/pallas_call | solution.py:565
  42.0 2.5 %shard_map.58 = (f32[1024,128]{1,0:T(8,128)}, f32[256,128]{1,0:T(8,128)}, f32[64,128]{1,0:T(8,128)}, f32[1]{0:T(128)}) custom-call(f32[1024,128]{1,0:T(8,128)S(1)} %get-tuple-element.10.xt, f32[1]{0:T(128)} %get-tuple-element.11.most), custom_call_target="tpu_custom_call" | custom-call | tf_op jit(solution)/shard_map/pallas_call | solution.py:593

commit v3 on v2

--- a/solution.py
+++ b/solution.py
@@ -27,9 +27,9 @@
 
 
 def kernel(
-    nz, plane, f_hbm, s_hbm, lines_ref, change_ref,
+    nz, plane, f_hbm, s_hbm, lines_ref, most_ref,
     fn, sn, h_ref, x_ref, d_ref, u_ref, ht, xt, vf, vb, edge,
-    s1a, r1a, s2a, r2a, s1b, r1b, s2b, r2b, s3, r3, pre, enter, xs, xr, paths,
+    s1a, r1a, s1b, r1b, s1c, r1c, s2a, r2a, s2b, r2b, s2c, r2c, s3, r3, s3c, r3c, pre, enter, xs, xr, paths,
     in_sem, send1, recv1, send2, recv2, send3, recv3, sendx, recvx,
 ):
     px, py = plane
@@ -53,12 +53,16 @@
             pltpu.make_async_copy(s_hbm.at[lines], sn.at[lines], in_sem.at[1, b]),
         )
 
+    x_at = [x] + [lax.rem(x + d, px) for d in range(1, px)]
+    y_at = [y] + [lax.rem(y + d, py) for d in range(1, py)]
+    z_at = [z] + [lax.rem(z + d, nz) for d in range(1, nz)]
+
     def slot(k):
         dx, dy = near_plane[k]
-        return lax.rem(x + dx, px) * py + lax.rem(y + dy, py)
+        return x_at[dx] * py + y_at[dy]
 
     def z_slot(k):
-        return lax.rem(z + near_z[k][0], nz)
+        return z_at[near_z[k][0]]
 
     barrier = pltpu.get_barrier_semaphore()
 
@@ -105,18 +109,20 @@
 
     lax.fori_loop(0, ROWS // 8, spread, 0)
 
-    def first_local(b, carry):
-        down, up, hd, hu, total = carry
+    def border_costs(b, carry):
+        down, up, hd, hu = carry
         for s in range(8):
             i = b * 8 + s
             h = h_ref[i]
             down = jnp.minimum(x_ref[i], down + (hd + h))
-            total = total + h
             hd = h
             h = h_ref[ROWS - 1 - i]
             up = jnp.minimum(x_ref[ROWS - 1 - i], up + (hu + h))
             hu = h
-        return (down, up, hd, hu, total)
+        return (down, up, hd, hu)
+
+    def add_rows(b, total):
+        return sum((h_ref[b * 8 + s] for s in range(8)), start=total)
 
     def second_local(b, carry):
         down, up, hd, hu, far_d, far_u, most = carry
@@ -146,160 +152,166 @@
         )
 
     my_z = jnp.full(part, z, jnp.int32)
-
-    def pick(k, new, old):
-        return jnp.where(my_z == k, new, old)
+    last = np_ - 1
+    not_hub = jnp.logical_not(hub)
+
+    def to_hub(to, got, n, k):
+        q = p if k == last else slot(k)
+        return remote(
+            to.at[q], got.at[core, p], send1.at[n, k], recv1.at[n, core, k], (z * np_ + q, HUB)
+        )
+
+    def send_to_hubs(to, got, n):
+        for k in range(last):
+            to_hub(to, got, n, k).start()
+
+        @pl.when(not_hub)
+        def _():
+            to_hub(to, got, n, last).start()
+
+    def sent_to_hubs(to, got, n):
+        for k in range(last):
+            to_hub(to, got, n, k).wait_send()
+
+        @pl.when(not_hub)
+        def _():
+            to_hub(to, got, n, last).wait_send()
+
+    def hub_has(to, got, n):
+        for item in range(to.shape[1]):
+            got[HUB, p, item] = to[p, item]
+        for k in range(np_ - 1, -1, -1):
+            for half in range(2):
+                if k == last and half == HUB:
+                    continue
+                remote(
+                    to.at[p], got.at[half, p], send1.at[n, k], recv1.at[n, half, k], (row, HUB)
+                ).wait_recv()
+
+    def along_z(source, got, n, k):
+        return remote(
+            source(k), got.at[z], send2.at[n, k], recv2.at[n, k], (z_slot(k) * np_ + p, HUB)
+        )
+
+    def by_side(to):
+        return lambda k: to.at[lax.div(z_slot(k) - z + nz, nz)]
+
+    def from_hub(source, got, n, half, k):
+        q = p if k == last else slot(k)
+        return remote(
+            source(half, q), got.at[p], send3.at[n, half, k], recv3.at[n, k], (z * np_ + q, half)
+        )
+
+    to_cores = [(half, k) for half in (1 - HUB, HUB) for k in range(np_) if (half, k) != (HUB, last)]
+
+    def cores_have(got, n):
+        def copy(k):
+            return remote(got.at[p], got.at[p], send3.at[n, HUB, k], recv3.at[n, k], (row, HUB))
+
+        @pl.when(not_hub)
+        def _():
+            copy(last).wait_recv()
+
+        for k in range(last - 1, -1, -1):
+            copy(k).wait_recv()
+
+    def plain(ref):
+        return lambda *_: ref
+
+    near = jnp.full(part, HUGE, jnp.float32)
+    none = jnp.zeros(part, jnp.float32)
+    rounds = ((s1a, r1a, s2a, r2a), (s1b, r1b, s2b, r2b))
 
     def vertical(step, window):
-        s1, r1, s2, r2 = ((s1a, r1a, s2a, r2a), (s1b, r1b, s2b, r2b))[step]
+        s1, r1, s2, r2 = rounds[step]
+        down, up, hd, hu = lax.fori_loop(0, ROWS // 8, border_costs, (huge, huge, zero, zero))
+        put(s1, 0, up + hu)
+        put(s1, 1, down + hd)
         if step == 0:
-            down, up, hd, hu, total = lax.fori_loop(
-                0, ROWS // 8, first_local, (huge, huge, zero, zero, zero)
-            )
-            values = (up + hu, down + hd, 2.0 * total)
-        else:
-            down, up, hd, hu, far_d, far_u, most = lax.fori_loop(
-                0, ROWS // 8, second_local, (huge, huge, zero, zero, -huge, -huge, zero)
-            )
-            values = (up + hu, down + hd, far_u - hu, far_d - hd, most)
-        items = len(values)
-        for item, value in enumerate(values):
-            put(s1, item, value)
-        if step == 0:
+            put(s1, 2, 2.0 * lax.fori_loop(0, ROWS // 8, add_rows, zero))
             wait_for_peers()
-        copies = []
-        for k in range(np_ - 1):
-            copy = remote(
-                s1.at[slot(k)], r1.at[p, :, core], send1.at[step, k], recv1.at[step, core, k],
-                (z * np_ + slot(k), HUB),
-            )
-            copy.start()
-            copies.append(copy)
-        last = np_ - 1
-        to_hub = remote(
-            s1.at[p], r1.at[p, :, core], send1.at[step, last], recv1.at[step, core, last], (row, HUB)
-        )
-
-        @pl.when(jnp.logical_not(hub))
-        def _():
-            to_hub.start()
-
+        send_to_hubs(s1, r1, step)
         window()
-
-        for copy in copies:
-            copy.wait_send()
-
-        @pl.when(jnp.logical_not(hub))
-        def _():
-            to_hub.wait_send()
-
         to, got = s3.at[step], r3.at[step]
 
         @pl.when(hub)
         def _():
-            for item in range(items):
-                r1[p, item, HUB] = s1[p, item]
-            for k in range(np_):
-                for half in range(2):
-                    if k == last and half == HUB:
-                        continue
-                    remote(
-                        s1.at[p], r1.at[p, :, half], send1.at[step, k], recv1.at[step, half, k], (row, HUB)
-                    ).wait_recv()
-            near = jnp.full(part, HUGE, jnp.float32)
-            none = jnp.zeros(part, jnp.float32)
-            b, a, s_down, s_up, far_d, far_u, most = near, near, none, none, -near, -near, none
+            hub_has(s1, r1, step)
+            b, a, s_down, s_up = near, near, none, none
             for q in range(np_):
-                r_a, r_b = r1[q, 0], r1[q, 1]
+                s = r1a[:, q, 2]
                 if step == 0:
-                    s = r1[q, 2]
                     pre[q, 2] = s_down
                     s_down = s_down + s
-                else:
-                    s = r1a[q, 2]
-                    most = jnp.maximum(most, jnp.maximum(far_d - r_a, r1[q, 2] - b))
-                    most = jnp.maximum(most, r1[q, 4])
-                    far_d = jnp.maximum(r1[q, 3], far_d - s)
                 pre[q, 0] = b
-                b = jnp.minimum(r_b, b + s)
+                b = jnp.minimum(r1[:, q, 1], b + s)
             for q in range(np_ - 1, -1, -1):
-                s = r1a[q, 2]
+                s = r1a[:, q, 2]
                 if step == 0:
                     pre[q, 3] = s_up
                     s_up = s_up + s
-                else:
-                    far_u = jnp.maximum(r1[q, 2], far_u - s)
                 pre[q, 1] = a
-                a = jnp.minimum(r1[q, 0], a + s)
-            values = (a, b, s_down) if step == 0 else (a, b, far_u, far_d, most)
-            for item, value in enumerate(values):
-                s2[item] = value
-            copies = []
+                a = jnp.minimum(r1[:, q, 0], a + s)
+            for side, value in enumerate((a, b)):
+                s2[side, 0] = value
+                if step == 0:
+                    s2[side, 1] = s_down
             for k in range(nz - 1):
-                copy = remote(
-                    s2, r2.at[z], send2.at[step, k], recv2.at[step, k], (z_slot(k) * np_ + p, HUB)
-                )
-                copy.start()
-                copies.append(copy)
-            for item in range(items):
-                r2[z, item] = values[item]
-            for copy in copies:
-                copy.wait()
-
-            b, a, far_d, most = near, near, -near, none
+                along_z(by_side(s2), r2, step, k).start()
+            r2[z, 0] = b
+            if step == 0:
+                r2[z, 1] = s_down
+            else:
+                hub_has(s1c, r1c, 2)
+                b, far_d, far_u, most = near, -near, -near, none
+                for q in range(np_):
+                    s, r_p = r1a[:, q, 2], r1c[:, q, 0]
+                    most = jnp.maximum(most, jnp.maximum(far_d - r1[:, q, 0], r_p - b))
+                    most = jnp.maximum(most, r1c[:, q, 2])
+                    far_d = jnp.maximum(r1c[:, q, 1], far_d - s)
+                    b = jnp.minimum(r1[:, q, 1], b + s)
+                for q in range(np_ - 1, -1, -1):
+                    far_u = jnp.maximum(r1c[:, q, 0], far_u - r1a[:, q, 2])
+                for item, value in enumerate((a, b, far_u, far_d, most)):
+                    s2c[item] = value
+                    r2c[z, item] = value
+                for k in range(nz - 1):
+                    along_z(plain(s2c), r2c, 2, k).start()
+            for k in range(nz - 2, -1, -1):
+                along_z(by_side(s2), r2, step, k).wait_recv()
             in_d, in_u = near, near
             for k in range(nz):
-                in_d = pick(k, b, in_d)
-                s = r2a[k, 2]
-                if step == 1:
-                    most = jnp.maximum(most, jnp.maximum(far_d - r2[k, 0], r2[k, 2] - b))
-                    most = jnp.maximum(most, r2[k, 4])
-                    far_d = jnp.maximum(r2[k, 3], far_d - s)
-                b = jnp.minimum(r2[k, 1], b + s)
+                in_d = jnp.where(my_z > k, jnp.minimum(r2[k, 0], in_d + r2a[k, 1]), in_d)
             for k in range(nz - 1, -1, -1):
-                in_u = pick(k, a, in_u)
-                a = jnp.minimum(r2[k, 0], a + r2a[k, 2])
-            most = jnp.maximum(most[0], most[1])
+                in_u = jnp.where(my_z < k, jnp.minimum(r2[k, 0], in_u + r2a[k, 1]), in_u)
             for q in range(np_):
-                to[q, 0] = jnp.minimum(pre[q, 0], in_d + pre[q, 2])
-                to[q, 1] = jnp.minimum(pre[q, 1], in_u + pre[q, 3])
-                to[q, 2, 0] = most
-                to[q, 2, 1] = most
-            copies = []
-            for half in (1 - HUB, HUB):
-                for k in range(np_):
-                    if k == last and half == HUB:
-                        continue
-                    q = p if k == last else slot(k)
-                    copy = remote(
-                        to.at[q, :, half], got.at[p], send3.at[step, half, k], recv3.at[step, k],
-                        (z * np_ + q, half),
-                    )
-                    copy.start()
-                    copies.append(copy)
-            for item in range(3):
-                got[p, item] = to[p, item, HUB]
-            for copy in copies:
-                copy.wait_send()
-
-        def from_hub(k):
-            return remote(
-                to.at[p, :, 0], got.at[p], send3.at[step, 0, k], recv3.at[step, k], (row, HUB)
-            )
-
-        for k in range(last):
-            from_hub(k).wait_recv()
-
-        @pl.when(jnp.logical_not(hub))
-        def _():
-            from_hub(last).wait_recv()
-
-        most = got[0, 2]
+                to[:, q, 0] = jnp.minimum(pre[q, 0], in_d + pre[q, 2])
+                to[:, q, 1] = jnp.minimum(pre[q, 1], in_u + pre[q, 3])
+            for half, k in to_cores:
+                from_hub(lambda h, q: to.at[h, q], got, step, half, k).start()
+            for item in range(2):
+                got[p, item] = to[HUB, p, item]
+            if step == 1:
+                for k in range(nz - 2, -1, -1):
+                    along_z(plain(s2c), r2c, 2, k).wait_recv()
+                b, far_d, most = near, -near, none
+                for k in range(nz):
+                    s = r2a[k, 1]
+                    most = jnp.maximum(most, jnp.maximum(far_d - r2c[k, 0], r2c[k, 2] - b))
+                    most = jnp.maximum(most, r2c[k, 4])
+                    far_d = jnp.maximum(r2c[k, 3], far_d - s)
+                    b = jnp.minimum(r2c[k, 1], b + s)
+                most = jnp.maximum(most[0], most[1])
+                s3c[...] = most
+                r3c[p] = most
+                for half, k in to_cores:
+                    from_hub(plain(s3c), r3c, 2, half, k).start()
+
+        cores_have(got, step)
         for q in range(np_):
             line = q * width
             for item in range(2):
                 enter[item, line // 8, line % 8 : line % 8 + width, :] = got[q, item]
-            most = jnp.maximum(most, got[q, 2])
 
         def final(b, carry):
             down, up, hd, hu = carry
@@ -316,7 +328,34 @@
             return (down, up, hd, hu)
 
         lax.fori_loop(0, ROWS // 8, final, (enter[0], enter[1], zero, zero))
-        return most
+
+    def second_window():
+        _, _, hd, hu, far_d, far_u, most = lax.fori_loop(
+            0, ROWS // 8, second_local, (huge, huge, zero, zero, -huge, -huge, zero)
+        )
+        put(s1c, 0, far_u - hu)
+        put(s1c, 1, far_d - hd)
+        put(s1c, 2, most)
+        send_to_hubs(s1c, r1c, 2)
+
+    def drain(step):
+        s1, r1, s2, r2 = rounds[step]
+        sent_to_hubs(s1, r1, step)
+        to, got = s3.at[step], r3.at[step]
+        if step == 1:
+            sent_to_hubs(s1c, r1c, 2)
+            cores_have(r3c, 2)
+
+        @pl.when(hub)
+        def _():
+            for k in range(nz - 1):
+                along_z(by_side(s2), r2, step, k).wait_send()
+                if step == 1:
+                    along_z(plain(s2c), r2c, 2, k).wait_send()
+            for half, k in to_cores:
+                from_hub(lambda h, q: to.at[h, q], got, step, half, k).wait_send()
+                if step == 1:
+                    from_hub(plain(s3c), r3c, 2, half, k).wait_send()
 
     lane = lax.broadcasted_iota(jnp.int32, (8, LANES), 1)
     sub = lax.broadcasted_iota(jnp.int32, (8, LANES), 0)
@@ -455,16 +494,16 @@
         return jnp.minimum(jnp.minimum(vf[rows, :], vb[rows, :]), edge[rows, :] + other[j : j + 1])
 
     vertical(0, measure)
-    other = horizontal(0, lambda: None)
+    other = horizontal(0, lambda: drain(0))
     for j in range(8):
         back = in_row(other, j).T
         x_ref[pl.ds((j // 4) * 16, 16), j % 4] = back.reshape(16, 8, LANES)
-    most = vertical(1, lambda: None)
-
-    def reduce_change():
-        change_ref[0] = jnp.max(most)
-
-    other = horizontal(1, reduce_change)
+    vertical(1, second_window)
+    other = horizontal(1, lambda: drain(1))
+    most = r3c[0]
+    for q in range(1, np_):
+        most = jnp.maximum(most, r3c[q])
+    most_ref[...] = most
 
     def merge(b, _):
         for t in range(16):
@@ -475,9 +514,11 @@
     lax.fori_loop(0, 8, merge, 0)
 
 
-def finish(xt, most, cost_hbm, one_hbm, two_hbm, change_ref, on, pairs, pool, o1, o2, out_sem):
+def finish(xt, most, cost_hbm, one_hbm, two_hbm, change_hbm, on, pairs, pool, o1, o2, change, out_sem):
     lane = lax.broadcasted_iota(jnp.int32, (8, LANES), 1)
-    outs = []
+    change[0] = jnp.max(most[...])
+    outs = [pltpu.make_async_copy(change, change_hbm, out_sem.at[4])]
+    outs[0].start()
     for j in range(8):
         back = xt[pl.ds(j, LANES, stride=8), :].T
         for r in range(16):
@@ -522,7 +563,6 @@
         o2[pl.ds(a, 8, stride=8), :] = jnp.where(lane < 64, low, high)
     out_two = pltpu.make_async_copy(o2, two_hbm, out_sem.at[1])
     out_two.start()
-    change_ref[0] = most[0]
     for out in outs:
         out.wait()
     out_one.wait()
@@ -548,7 +588,6 @@
     f32 = jnp.float32
     anywhere = pl.BlockSpec(memory_space=pltpu.HBM)
     in_vmem = pl.BlockSpec(memory_space=pltpu.VMEM)
-    in_smem = pl.BlockSpec(memory_space=pltpu.SMEM)
     field = pltpu.VMEM((ROWS, 4, 8, LANES), f32)
     flat = pltpu.VMEM((ROWS * CHUNKS, LANES), f32)
     dma = pltpu.SemaphoreType.DMA
@@ -560,30 +599,34 @@
         return pltpu.with_memory_space_constraint(lines_of(block), pltpu.HBM)
 
     rounds = []
-    for items in (3, 5):
-        rounds += [message((np_,), items), message((np_,), items, 2), message((), items, 2), message((nz,), items, 2)]
-    lines, change = pl.pallas_call(
+    for items in (3, 2, 3):
+        rounds += [message((np_,), items), message((2, np_), items)]
+    for sides, items in (((2,), 2), ((2,), 1), ((), 5)):
+        rounds += [message(sides, items, 2), message((nz,), items, 2)]
+    lines, most = pl.pallas_call(
         functools.partial(kernel, nz, plane),
-        out_shape=(jax.ShapeDtypeStruct((1024, LANES), f32), jax.ShapeDtypeStruct((1,), f32)),
+        out_shape=(jax.ShapeDtypeStruct((1024, LANES), f32), jax.ShapeDtypeStruct((width, LANES), f32)),
         in_specs=[anywhere, anywhere],
-        out_specs=(in_vmem, in_smem),
+        out_specs=(in_vmem, in_vmem),
         scratch_shapes=[
             flat,
             pltpu.VMEM((ROWS * CHUNKS, LANES), jnp.int32),
             field, field, field, field,
             flat, flat, flat, flat, flat,
             *rounds,
-            message((2, np_), 3, 2),
-            message((2, np_), 3),
+            message((2, 2, np_), 2),
+            message((2, np_), 2),
+            pltpu.VMEM((width, LANES), f32),
+            pltpu.VMEM((np_, width, LANES), f32),
             message((np_,), 4, 2),
             pltpu.VMEM((2, 4, 8, LANES), f32),
             pltpu.VMEM((2, 8, LANES), f32),
             pltpu.VMEM((2, 8, LANES), f32),
             pltpu.VMEM((30, 8, LANES), f32),
             dma((2, 4)),
-            dma((2, np_)), dma((2, 2, np_)),
-            dma((2, nz)), dma((2, nz)),
-            dma((2, 2, np_)), dma((2, np_)),
+            dma((3, np_)), dma((3, 2, np_)),
+            dma((3, nz)), dma((3, nz)),
+            dma((3, 2, np_)), dma((3, np_)),
             dma((2,)), dma((2,)),
         ],
         compiler_params=pltpu.CompilerParams(
@@ -598,18 +641,19 @@
             jax.ShapeDtypeStruct((64, LANES), f32),
             jax.ShapeDtypeStruct((1,), f32),
         ),
-        in_specs=[in_vmem, in_smem],
-        out_specs=(anywhere, anywhere, anywhere, in_smem),
+        in_specs=[in_vmem, in_vmem],
+        out_specs=(anywhere,) * 4,
         scratch_shapes=[
             flat,
             pltpu.VMEM((512, LANES), f32),
             pltpu.VMEM((24, 4, 8, LANES), f32),
             pltpu.VMEM((256, LANES), f32),
             pltpu.VMEM((64, LANES), f32),
-            dma((4,)),
+            pltpu.SMEM((1,), f32),
+            dma((5,)),
         ],
         compiler_params=pltpu.CompilerParams(vmem_limit_bytes=16 * 1024 * 1024),
-    )(lines, change)
+    )(lines, most)
     return (block_of(cost, 32), block_of(one, 16), block_of(two, 8), change)
 
 

time: 44.5 us -> 42.9 us (0.964)
  Pallas kernels: 43.8 us -> 42.1 us
    pallas_call x1, Pallas kernels: 2.46 us -> 1.35 us  [shards(): pl.pallas_call(finish, out_shape=(jax.ShapeDtypeStruct((1024, LANES), f32...]
    pallas_call x1, Pallas kernels: 41.3 us -> 40.8 us  [shards(): pl.pallas_call(functools.partial(kernel, nz, plane), out_shape=(jax.Shape...]
where the time goes in v3:
time: 42.9 us; the launch traced here: 42.7 us
  Pallas kernels  42.1 us (98%)
  between operations  0.64 us (1%)
    pallas_call x1, Pallas kernels, shards(): pl.pallas_call(functools.partial(kernel, nz, plane), out_shape=(jax.Shape...  40.8 us
    pallas_call x1, Pallas kernels, shards(): pl.pallas_call(finish, out_shape=(jax.ShapeDtypeStruct((1024, LANES), f32...  1.35 us

profile of v3, /device:TPU:1, one launch (start us, length us, event | category | flops | bytes accessed | tf_op | source)
XLA Modules:
  0.0 42.7 jit_solution(5313785716061359914)
XLA Ops:
  0.6 40.8 %shard_map.57 = (f32[1024,128]{1,0:T(8,128)S(1)}, f32[2,128]{1,0:T(2,128)S(1)}) custom-call(f32[1024,128]{1,0:T(8,128)} %bitcast.25, s32[1024,128]{1,0:T(8,128)} %bitcast.26), custom_call_target="tpu_custom_call" | custom-call | tf_op jit(solution)/shard_map/pallas_call | solution.py:606
  41.4 1.3 %shard_map.58 = (f32[1024,128]{1,0:T(8,128)}, f32[256,128]{1,0:T(8,128)}, f32[64,128]{1,0:T(8,128)}, f32[1]{0:T(128)}) custom-call(f32[1024,128]{1,0:T(8,128)S(1)} %get-tuple-element.10.xt, f32[2,128]{1,0:T(2,128)S(1)} %get-tuple-element.11.most), custom_call_target="tpu_custom_call" | custom-call | tf_op jit(solution)/shard_map/pallas_call | solution.py:636

commit v4 on v3

--- a/solution.py
+++ b/solution.py
@@ -53,6 +53,10 @@
             pltpu.make_async_copy(s_hbm.at[lines], sn.at[lines], in_sem.at[1, b]),
         )
 
+    for b in range(4):
+        for copy in in_copies(b):
+            copy.start()
+
     x_at = [x] + [lax.rem(x + d, px) for d in range(1, px)]
     y_at = [y] + [lax.rem(y + d, py) for d in range(1, py)]
     z_at = [z] + [lax.rem(z + d, nz) for d in range(1, nz)]
@@ -69,26 +73,19 @@
     def greet(device):
         pl.semaphore_signal(barrier, inc=1, device_id=device, device_id_type=MESH)
 
-    for k in range(np_ - 1):
-        greet((z * np_ + slot(k), HUB))
-
     @pl.when(hub)
     def _():
         for k in range(np_ - 1):
+            greet((z * np_ + slot(k), HUB))
+            if k < nz - 1:
+                greet((z_slot(k) * np_ + p, HUB))
             greet((z * np_ + slot(k), 1 - HUB))
-        for k in range(nz - 1):
-            greet((z_slot(k) * np_ + p, HUB))
-
-    greet((row, other_core))
-
-    for b in range(4):
-        for copy in in_copies(b):
-            copy.start()
+        greet((row, 1 - HUB))
 
     def wait_for_peers():
         @pl.when(hub)
         def _():
-            pl.semaphore_wait(barrier, 2 * (np_ - 1) + nz)
+            pl.semaphore_wait(barrier, np_ - 1 + nz - 1)
 
         @pl.when(jnp.logical_not(hub))
         def _():
@@ -411,15 +408,18 @@
         paths[28] = before
         paths[29] = after
 
-        def border(i, path):
-            i = core * i + other_core * (LANES - 1 - i)
-            h = ht[at(i), :]
-            edge[at(i), :] = path + h
-            return path + 2.0 * h
+        def border(b, path):
+            for t in range(8):
+                i = b * 8 + t
+                i = core * i + other_core * (LANES - 1 - i)
+                h = ht[at(i), :]
+                edge[at(i), :] = path + h
+                path = path + 2.0 * h
+            return path
 
         first = jnp.full((8, LANES), core, jnp.int32) == 0
         lax.fori_loop(
-            0, LANES, border, jnp.where(first, paths[27] + paths[29], paths[26] + paths[28])
+            0, LANES // 8, border, jnp.where(first, paths[27] + paths[29], paths[26] + paths[28])
         )
 
     def scan_all(c, path, axis, size, place, forward):

time: 42.9 us -> 42.6 us (level)
  no operation moved by 1% of the time
where the time goes in v4:
time: 42.6 us; the launch traced here: 42.5 us
  Pallas kernels  41.9 us (98%)
  between operations  0.64 us (2%)
    pallas_call x1, Pallas kernels, shards(): pl.pallas_call(functools.partial(kernel, nz, plane), out_shape=(jax.Shape...  40.5 us
    pallas_call x1, Pallas kernels, shards(): pl.pallas_call(finish, out_shape=(jax.ShapeDtypeStruct((1024, LANES), f32...  1.35 us

profile of v4, /device:TPU:1, one launch (start us, length us, event | category | flops | bytes accessed | tf_op | source)
XLA Modules:
  0.0 42.5 jit_solution(7364721776100589471)
XLA Ops:
  0.6 40.5 %shard_map.57 = (f32[1024,128]{1,0:T(8,128)S(1)}, f32[2,128]{1,0:T(2,128)S(1)}) custom-call(f32[1024,128]{1,0:T(8,128)} %bitcast.25, s32[1024,128]{1,0:T(8,128)} %bitcast.26), custom_call_target="tpu_custom_call" | custom-call | tf_op jit(solution)/shard_map/pallas_call | solution.py:606
  41.2 1.3 %shard_map.58 = (f32[1024,128]{1,0:T(8,128)}, f32[256,128]{1,0:T(8,128)}, f32[64,128]{1,0:T(8,128)}, f32[1]{0:T(128)}) custom-call(f32[1024,128]{1,0:T(8,128)S(1)} %get-tuple-element.10.xt, f32[2,128]{1,0:T(2,128)S(1)} %get-tuple-element.11.most), custom_call_target="tpu_custom_call" | custom-call | tf_op jit(solution)/shard_map/pallas_call | solution.py:636

commit v5 on v4

--- a/solution.py
+++ b/solution.py
@@ -46,16 +46,12 @@
     near_plane = far_first(plane)
     near_z = far_first((nz,))
 
-    def in_copies(b):
-        lines = pl.ds(pl.multiple_of(b * 256, 256), 256)
-        return (
-            pltpu.make_async_copy(f_hbm.at[lines], fn.at[lines], in_sem.at[0, b]),
-            pltpu.make_async_copy(s_hbm.at[lines], sn.at[lines], in_sem.at[1, b]),
-        )
-
-    for b in range(4):
-        for copy in in_copies(b):
-            copy.start()
+    loads = (
+        pltpu.make_async_copy(f_hbm, fn, in_sem.at[0]),
+        pltpu.make_async_copy(s_hbm, sn, in_sem.at[1]),
+    )
+    for load in loads:
+        load.start()
 
     x_at = [x] + [lax.rem(x + d, px) for d in range(1, px)]
     y_at = [y] + [lax.rem(y + d, py) for d in range(1, py)]
@@ -95,8 +91,6 @@
     zero = jnp.zeros(tile, jnp.float32)
 
     def spread(b, _):
-        for copy in in_copies(b):
-            copy.wait()
         for s in range(8):
             for g in range(4):
                 lines = pl.ds((b * 32 + g * 8) * 8 + s, 8, stride=8)
@@ -104,6 +98,8 @@
                 x_ref[b * 8 + s, g] = jnp.where(sn[lines, :] == 1, 0.0, HUGE)
         return 0
 
+    for load in loads:
+        load.wait()
     lax.fori_loop(0, ROWS // 8, spread, 0)
 
     def border_costs(b, carry):
@@ -155,7 +151,7 @@
     def to_hub(to, got, n, k):
         q = p if k == last else slot(k)
         return remote(
-            to.at[q], got.at[core, p], send1.at[n, k], recv1.at[n, core, k], (z * np_ + q, HUB)
+            to.at[q], got.at[core, p], send1.at[n], recv1.at[n, core], (z * np_ + q, HUB)
         )
 
     def send_to_hubs(to, got, n):
@@ -166,28 +162,30 @@
         def _():
             to_hub(to, got, n, last).start()
 
+    def arrived(ref, sem):
+        remote(ref, ref, send1.at[0], sem, (row, HUB)).wait_recv()
+
+    def sent(ref, sem):
+        remote(ref, ref, sem, recv1.at[0, 0], (row, HUB)).wait_send()
+
     def sent_to_hubs(to, got, n):
-        for k in range(last):
-            to_hub(to, got, n, k).wait_send()
+        @pl.when(hub)
+        def _():
+            sent(to.at[pl.ds(0, last)], send1.at[n])
 
         @pl.when(not_hub)
         def _():
-            to_hub(to, got, n, last).wait_send()
+            sent(to, send1.at[n])
 
     def hub_has(to, got, n):
         for item in range(to.shape[1]):
             got[HUB, p, item] = to[p, item]
-        for k in range(np_ - 1, -1, -1):
-            for half in range(2):
-                if k == last and half == HUB:
-                    continue
-                remote(
-                    to.at[p], got.at[half, p], send1.at[n, k], recv1.at[n, half, k], (row, HUB)
-                ).wait_recv()
+        arrived(got.at[HUB, pl.ds(0, last)], recv1.at[n, HUB])
+        arrived(got.at[1 - HUB], recv1.at[n, 1 - HUB])
 
     def along_z(source, got, n, k):
         return remote(
-            source(k), got.at[z], send2.at[n, k], recv2.at[n, k], (z_slot(k) * np_ + p, HUB)
+            source(k), got.at[z], send2.at[n], recv2.at[n], (z_slot(k) * np_ + p, HUB)
         )
 
     def by_side(to):
@@ -196,21 +194,23 @@
     def from_hub(source, got, n, half, k):
         q = p if k == last else slot(k)
         return remote(
-            source(half, q), got.at[p], send3.at[n, half, k], recv3.at[n, k], (z * np_ + q, half)
+            source(half, q), got.at[p], send3.at[n, half], recv3.at[n], (z * np_ + q, half)
         )
 
     to_cores = [(half, k) for half in (1 - HUB, HUB) for k in range(np_) if (half, k) != (HUB, last)]
 
     def cores_have(got, n):
-        def copy(k):
-            return remote(got.at[p], got.at[p], send3.at[n, HUB, k], recv3.at[n, k], (row, HUB))
+        @pl.when(hub)
+        def _():
+            arrived(got.at[pl.ds(0, last)], recv3.at[n])
 
         @pl.when(not_hub)
         def _():
-            copy(last).wait_recv()
-
-        for k in range(last - 1, -1, -1):
-            copy(k).wait_recv()
+            arrived(got, recv3.at[n])
+
+    def sent_to_cores(got, n):
+        sent(got, send3.at[n, 1 - HUB])
+        sent(got.at[pl.ds(0, last)], send3.at[n, HUB])
 
     def plain(ref):
         return lambda *_: ref
@@ -274,8 +274,7 @@
                     r2c[z, item] = value
                 for k in range(nz - 1):
                     along_z(plain(s2c), r2c, 2, k).start()
-            for k in range(nz - 2, -1, -1):
-                along_z(by_side(s2), r2, step, k).wait_recv()
+            arrived(r2.at[pl.ds(0, nz - 1)], recv2.at[step])
             in_d, in_u = near, near
             for k in range(nz):
                 in_d = jnp.where(my_z > k, jnp.minimum(r2[k, 0], in_d + r2a[k, 1]), in_d)
@@ -289,8 +288,7 @@
             for item in range(2):
                 got[p, item] = to[HUB, p, item]
             if step == 1:
-                for k in range(nz - 2, -1, -1):
-                    along_z(plain(s2c), r2c, 2, k).wait_recv()
+                arrived(r2c.at[pl.ds(0, nz - 1)], recv2.at[2])
                 b, far_d, most = near, -near, none
                 for k in range(nz):
                     s = r2a[k, 1]
@@ -345,14 +343,11 @@
 
         @pl.when(hub)
         def _():
-            for k in range(nz - 1):
-                along_z(by_side(s2), r2, step, k).wait_send()
-                if step == 1:
-                    along_z(plain(s2c), r2c, 2, k).wait_send()
-            for half, k in to_cores:
-                from_hub(lambda h, q: to.at[h, q], got, step, half, k).wait_send()
-                if step == 1:
-                    from_hub(plain(s3c), r3c, 2, half, k).wait_send()
+            sent(r2.at[pl.ds(0, nz - 1)], send2.at[step])
+            sent_to_cores(got, step)
+            if step == 1:
+                sent(r2c.at[pl.ds(0, nz - 1)], send2.at[2])
+                sent_to_cores(r3c, 2)
 
     lane = lax.broadcasted_iota(jnp.int32, (8, LANES), 1)
     sub = lax.broadcasted_iota(jnp.int32, (8, LANES), 0)
@@ -623,10 +618,10 @@
             pltpu.VMEM((2, 8, LANES), f32),
             pltpu.VMEM((2, 8, LANES), f32),
             pltpu.VMEM((30, 8, LANES), f32),
-            dma((2, 4)),
-            dma((3, np_)), dma((3, 2, np_)),
-            dma((3, nz)), dma((3, nz)),
-            dma((3, 2, np_)), dma((3, np_)),
+            dma((2,)),
+            dma((3,)), dma((3, 2)),
+            dma((3,)), dma((3,)),
+            dma((3, 2)), dma((3,)),
             dma((2,)), dma((2,)),
         ],
         compiler_params=pltpu.CompilerParams(

time: 42.6 us -> 39.7 us (0.932)
  Pallas kernels: 41.9 us -> 39 us
    pallas_call x1, Pallas kernels: 40.5 us -> 37.6 us  [shards(): pl.pallas_call(functools.partial(kernel, nz, plane), out_shape=(jax.Shape...]
where the time goes in v5:
time: 39.7 us; the launch traced here: 39.6 us
  Pallas kernels  39 us (98%)
  between operations  0.64 us (2%)
    pallas_call x1, Pallas kernels, shards(): pl.pallas_call(functools.partial(kernel, nz, plane), out_shape=(jax.Shape...  37.6 us
    pallas_call x1, Pallas kernels, shards(): pl.pallas_call(finish, out_shape=(jax.ShapeDtypeStruct((1024, LANES), f32...  1.35 us

profile of v5, /device:TPU:1, one launch (start us, length us, event | category | flops | bytes accessed | tf_op | source)
XLA Modules:
  0.0 39.6 jit_solution(14375968824446909321)
XLA Ops:
  0.6 37.6 %shard_map.57 = (f32[1024,128]{1,0:T(8,128)S(1)}, f32[2,128]{1,0:T(2,128)S(1)}) custom-call(f32[1024,128]{1,0:T(8,128)} %bitcast.25, s32[1024,128]{1,0:T(8,128)} %bitcast.26), custom_call_target="tpu_custom_call" | custom-call | tf_op jit(solution)/shard_map/pallas_call | solution.py:601
  38.3 1.3 %shard_map.58 = (f32[1024,128]{1,0:T(8,128)}, f32[256,128]{1,0:T(8,128)}, f32[64,128]{1,0:T(8,128)}, f32[1]{0:T(128)}) custom-call(f32[1024,128]{1,0:T(8,128)S(1)} %get-tuple-element.10.xt, f32[2,128]{1,0:T(2,128)S(1)} %get-tuple-element.11.most), custom_call_target="tpu_custom_call" | custom-call | tf_op jit(solution)/shard_map/pallas_call | solution.py:631

commit v6 on v5

--- a/solution.py
+++ b/solution.py
@@ -151,7 +151,7 @@
     def to_hub(to, got, n, k):
         q = p if k == last else slot(k)
         return remote(
-            to.at[q], got.at[core, p], send1.at[n], recv1.at[n, core], (z * np_ + q, HUB)
+            to.at[q], got.at[core, p], send1.at[n // 2], recv1.at[n, core], (z * np_ + q, HUB)
         )
 
     def send_to_hubs(to, got, n):
@@ -171,11 +171,11 @@
     def sent_to_hubs(to, got, n):
         @pl.when(hub)
         def _():
-            sent(to.at[pl.ds(0, last)], send1.at[n])
+            sent(to.at[pl.ds(0, last)], send1.at[n // 2])
 
         @pl.when(not_hub)
         def _():
-            sent(to, send1.at[n])
+            sent(to, send1.at[n // 2])
 
     def hub_has(to, got, n):
         for item in range(to.shape[1]):
@@ -185,7 +185,7 @@
 
     def along_z(source, got, n, k):
         return remote(
-            source(k), got.at[z], send2.at[n], recv2.at[n], (z_slot(k) * np_ + p, HUB)
+            source(k), got.at[z], send2.at[n // 2], recv2.at[n], (z_slot(k) * np_ + p, HUB)
         )
 
     def by_side(to):
@@ -194,10 +194,10 @@
     def from_hub(source, got, n, half, k):
         q = p if k == last else slot(k)
         return remote(
-            source(half, q), got.at[p], send3.at[n, half], recv3.at[n], (z * np_ + q, half)
+            source(half, q), got.at[p], send3.at[n // 2, half], recv3.at[n], (z * np_ + q, half)
         )
 
-    to_cores = [(half, k) for half in (1 - HUB, HUB) for k in range(np_) if (half, k) != (HUB, last)]
+    to_cores = [(half, k) for k in range(np_) for half in (1 - HUB, HUB) if (half, k) != (HUB, last)]
 
     def cores_have(got, n):
         @pl.when(hub)
@@ -209,8 +209,8 @@
             arrived(got, recv3.at[n])
 
     def sent_to_cores(got, n):
-        sent(got, send3.at[n, 1 - HUB])
-        sent(got.at[pl.ds(0, last)], send3.at[n, HUB])
+        sent(got, send3.at[n // 2, 1 - HUB])
+        sent(got.at[pl.ds(0, last)], send3.at[n // 2, HUB])
 
     def plain(ref):
         return lambda *_: ref
@@ -343,10 +343,10 @@
 
         @pl.when(hub)
         def _():
-            sent(r2.at[pl.ds(0, nz - 1)], send2.at[step])
+            sent(r2.at[pl.ds(0, nz - 1)], send2.at[0])
             sent_to_cores(got, step)
             if step == 1:
-                sent(r2c.at[pl.ds(0, nz - 1)], send2.at[2])
+                sent(r2c.at[pl.ds(0, nz - 1)], send2.at[1])
                 sent_to_cores(r3c, 2)
 
     lane = lax.broadcasted_iota(jnp.int32, (8, LANES), 1)
@@ -472,7 +472,7 @@
         gbc, gb_all = scan_all(b_all, group_path, 0, 4, outer, False)
         first = jnp.full((8, LANES), core, jnp.int32) == 0
         xs[step] = jnp.where(first, gf_all, gb_all)
-        copy = remote(xs.at[step], xr.at[step], sendx.at[step], recvx.at[step], (row, other_core))
+        copy = remote(xs.at[step], xr.at[step], sendx.at[0], recvx.at[step], (row, other_core))
         copy.start()
         in_f = [jnp.minimum(fc, gfc + paths[26])]
         in_b = [jnp.minimum(bc, gbc + paths[27])]
@@ -480,13 +480,21 @@
             in_f.append(jnp.minimum(right[k], in_f[k] + paths[k]))
             in_b.append(jnp.minimum(left[-1 - k], in_b[k] + paths[PARTS - 1 - k]))
         sweep(tuple(in_f), tuple(in_b[::-1]), True)
+
+        def merge(b, _):
+            for t in range(16):
+                i = at(b * 16 + t)
+                xt[i, :] = jnp.minimum(vf[i, :], vb[i, :])
+            return 0
+
+        lax.fori_loop(0, 8, merge, 0)
         window()
         copy.wait()
         return xr[step]
 
     def in_row(other, j):
         rows = pl.ds(j, LANES, stride=8)
-        return jnp.minimum(jnp.minimum(vf[rows, :], vb[rows, :]), edge[rows, :] + other[j : j + 1])
+        return jnp.minimum(xt[rows, :], edge[rows, :] + other[j : j + 1])
 
     vertical(0, measure)
     other = horizontal(0, lambda: drain(0))
@@ -503,7 +511,7 @@
     def merge(b, _):
         for t in range(16):
             i = at(b * 16 + t)
-            lines_ref[i, :] = jnp.minimum(jnp.minimum(vf[i, :], vb[i, :]), edge[i, :] + other)
+            lines_ref[i, :] = jnp.minimum(xt[i, :], edge[i, :] + other)
         return 0
 
     lax.fori_loop(0, 8, merge, 0)
@@ -619,10 +627,10 @@
             pltpu.VMEM((2, 8, LANES), f32),
             pltpu.VMEM((30, 8, LANES), f32),
             dma((2,)),
-            dma((3,)), dma((3, 2)),
-            dma((3,)), dma((3,)),
-            dma((3, 2)), dma((3,)),
-            dma((2,)), dma((2,)),
+            dma((2,)), dma((3, 2)),
+            dma((2,)), dma((3,)),
+            dma((2, 2)), dma((3,)),
+            dma((1,)), dma((2,)),
         ],
         compiler_params=pltpu.CompilerParams(
             collective_id=0, has_side_effects=True, vmem_limit_bytes=16 * 1024 * 1024

time: 39.7 us -> 39.6 us (level)
  no operation moved by 1% of the time
where the time goes in v6:
time: 39.6 us; the launch traced here: 39.5 us
  Pallas kernels  38.9 us (98%)
  between operations  0.64 us (2%)
    pallas_call x1, Pallas kernels, shards(): pl.pallas_call(functools.partial(kernel, nz, plane), out_shape=(jax.Shape...  37.5 us
    pallas_call x1, Pallas kernels, shards(): pl.pallas_call(finish, out_shape=(jax.ShapeDtypeStruct((1024, LANES), f32...  1.35 us

profile of v6, /device:TPU:1, one launch (start us, length us, event | category | flops | bytes accessed | tf_op | source)
XLA Modules:
  0.0 39.5 jit_solution(2635739240115116202)
XLA Ops:
  0.6 37.5 %shard_map.57 = (f32[1024,128]{1,0:T(8,128)S(1)}, f32[2,128]{1,0:T(2,128)S(1)}) custom-call(f32[1024,128]{1,0:T(8,128)} %bitcast.25, s32[1024,128]{1,0:T(8,128)} %bitcast.26), custom_call_target="tpu_custom_call" | custom-call | tf_op jit(solution)/shard_map/pallas_call | solution.py:609
  38.2 1.3 %shard_map.58 = (f32[1024,128]{1,0:T(8,128)}, f32[256,128]{1,0:T(8,128)}, f32[64,128]{1,0:T(8,128)}, f32[1]{0:T(128)}) custom-call(f32[1024,128]{1,0:T(8,128)S(1)} %get-tuple-element.10.xt, f32[2,128]{1,0:T(2,128)S(1)} %get-tuple-element.11.most), custom_call_target="tpu_custom_call" | custom-call | tf_op jit(solution)/shard_map/pallas_call | solution.py:639
